TPU v7x, 32 devices: a whole 2x2x4 slice. The times are simulated.
32 devices in a mesh: dp: 2 (over x), row: 4 (over z), col: 4 (over y, core).
Axes of the slice: x: 2, y: 2, z: 4, core: 2. Of those that a mesh axis runs over, the one named last changes fastest.
Arguments:
- x: bfloat16 [2048, 1024], P(('dp', 'row', 'col')), parts along dimension 0
- route_idx: int32 [2048, 8], P(('dp', 'row', 'col')), parts along dimension 0
- gates: float32 [2048, 8], P(('dp', 'row', 'col')), parts along dimension 0
- w1: bfloat16 [128, 1024, 384], P(('row', 'col'))
- w3: bfloat16 [128, 1024, 384], P(('row', 'col'))
- w2: bfloat16 [128, 384, 1024], P(('row', 'col'))
- dy: bfloat16 [2048, 1024], P(('dp', 'row', 'col')), parts along dimension 0
Outputs:
- output 1: bfloat16 [2048, 1024], P(('dp', 'row', 'col')), parts along dimension 0
- output 2: bfloat16 [2048, 1024], P(('dp', 'row', 'col')), parts along dimension 0
- output 3: float32 [2048, 8], P(('dp', 'row', 'col')), parts along dimension 0
- output 4: float32 [256, 1024, 384], P(('dp', 'row', 'col')), parts along dimension 0
- output 5: float32 [256, 1024, 384], P(('dp', 'row', 'col')), parts along dimension 0
- output 6: float32 [256, 384, 1024], P(('dp', 'row', 'col')), parts along dimension 0
There are 2 independent parts. A program takes and returns all parts, laid end to end along the dimension named above; an argument that names none is the same for every part.
All inputs are finite; a program needn't handle non-finite values.
Results may differ from a plain program's by a relative error of at most 0.00121.
Values are sent between devices in bfloat16 or wider.
A program may use at most 1 GiB of HBM per device.

v0:
```python
import jax
import jax.numpy as jnp
from jax import lax
from jax.sharding import PartitionSpec as P


def slot_positions(ridx, ne, cap):
    tok, top = ridx.shape
    n = tok * top
    ef = ridx.reshape(n)
    order = jnp.argsort(ef, stable=True).astype(jnp.int32)
    es = ef[order]
    first = jnp.searchsorted(es, es, side='left').astype(jnp.int32)
    rank = jnp.arange(n, dtype=jnp.int32) - first
    pos = jnp.zeros((n,), jnp.int32).at[order].set(es * cap + rank)
    inv = jnp.full((ne * cap,), n, jnp.int32).at[pos].set(jnp.arange(n, dtype=jnp.int32))
    return pos, inv


def to_experts(buf, nd, el, cap):
    d = buf.shape[-1]
    return buf.reshape(nd, el, cap, d).transpose(1, 0, 2, 3).reshape(el, nd * cap, d)


def from_experts(buf, nd, el, cap):
    d = buf.shape[-1]
    return buf.reshape(el, nd, cap, d).transpose(1, 0, 2, 3).reshape(nd, el * cap, d)


def expert_forward(xe, w1, w3, w2):
    u = jnp.einsum('ecd,edf->ecf', xe, w1, preferred_element_type=jnp.float32).astype(jnp.bfloat16)
    v = jnp.einsum('ecd,edf->ecf', xe, w3, preferred_element_type=jnp.float32).astype(jnp.bfloat16)
    uf = u.astype(jnp.float32)
    a = (uf * jax.nn.sigmoid(uf) * v.astype(jnp.float32)).astype(jnp.bfloat16)
    o = jnp.einsum('ecf,efd->ecd', a, w2, preferred_element_type=jnp.float32).astype(jnp.bfloat16)
    return u, v, a, o


def expert_backward(xe, u, v, a, doe, w1, w3, w2):
    gw2 = jnp.einsum('ecf,ecd->efd', a, doe, preferred_element_type=jnp.float32)
    da = jnp.einsum('ecd,efd->ecf', doe, w2, preferred_element_type=jnp.float32)
    uf = u.astype(jnp.float32)
    vf = v.astype(jnp.float32)
    sg = jax.nn.sigmoid(uf)
    du = (da * vf * sg * (1.0 + uf * (1.0 - sg))).astype(jnp.bfloat16)
    dv = (da * uf * sg).astype(jnp.bfloat16)
    gw1 = jnp.einsum('ecd,ecf->edf', xe, du, preferred_element_type=jnp.float32)
    gw3 = jnp.einsum('ecd,ecf->edf', xe, dv, preferred_element_type=jnp.float32)
    dxe = (jnp.einsum('ecf,edf->ecd', du, w1, preferred_element_type=jnp.float32) + jnp.einsum('ecf,edf->ecd', dv, w3, preferred_element_type=jnp.float32)).astype(jnp.bfloat16)
    return gw1, gw3, gw2, dxe


def solution(mesh):
    nd = mesh.shape['row'] * mesh.shape['col']
    grp = ('row', 'col')
    tspec = P(('dp', 'row', 'col'), None)
    wspec = P(grp, None, None)
    gspec = P(('dp', 'row', 'col'), None, None)

    def exchange(buf):
        return lax.all_to_all(buf, grp, 0, 0, tiled=True)

    def local(x, ridx, gates, w1, w3, w2, dy):
        tok, d = x.shape
        top = ridx.shape[1]
        el = w1.shape[0]
        ne = el * nd
        cap = (4 * tok * top + ne - 1) // ne
        n = tok * top
        pos, inv = slot_positions(ridx, ne, cap)
        zrow = jnp.zeros((1, d), x.dtype)
        send = jnp.concatenate([x, zrow])[inv // top].reshape(nd, el * cap, d)
        xe = to_experts(exchange(send), nd, el, cap)
        u, v, a, oe = expert_forward(xe, w1, w3, w2)
        ret = exchange(from_experts(oe, nd, el, cap)).reshape(ne * cap, d)
        ob = ret[pos].reshape(tok, top, d)
        y = jnp.sum(gates[:, :, None] * ob.astype(jnp.float32), axis=1).astype(jnp.bfloat16)
        dgates = jnp.einsum('td,tjd->tj', dy, ob, preferred_element_type=jnp.float32)
        do = (gates[:, :, None] * dy[:, None, :].astype(jnp.float32)).astype(jnp.bfloat16).reshape(n, d)
        dsend = jnp.concatenate([do, zrow])[inv].reshape(nd, el * cap, d)
        doe = to_experts(exchange(dsend), nd, el, cap)
        gw1, gw3, gw2, dxe = expert_backward(xe, u, v, a, doe, w1, w3, w2)
        dret = exchange(from_experts(dxe, nd, el, cap)).reshape(ne * cap, d)
        dx = jnp.sum(dret[pos].reshape(tok, top, d).astype(jnp.float32), axis=1).astype(jnp.bfloat16)
        return y, dx, dgates, gw1, gw3, gw2

    return jax.shard_map(local, mesh=mesh, in_specs=(tspec, tspec, tspec, wspec, wspec, wspec, tspec), out_specs=(tspec, tspec, tspec, gspec, gspec, gspec), check_vma=False)
```

profile of v0, /device:TPU:13, one launch (start us, length us, event | category | flops | bytes accessed | tf_op | source)
XLA Modules:
  0.0 458.0 jit_solution(10989944659936483104)
XLA Ops:
  0.6 0.8 copy.18
  1.4 0.1 reshape.63
  1.5 3.8 sort.17
  5.3 3.5 gather_fusion.1
  8.8 0.0 copy-start.5
  8.8 35.9 %while.25 = (s32[]{:T(128)}, u32[512]{0:T(512)S(1)}, u32[512]{0:T(512)S(1)}, s32[512]{0:T(512)S(1)}, s32[]{:T(128)}, /*index=5*/s32[]{:T(128)}, s32[]{}) while((s32[]{:T(128)}, u32[512]{0:T(512)S(1)}, u32[512]{0:T(512)S(1)}, s32[512]{0:T(512)S(1)}, s32[]{:T(128)}, /*index=5*/s32[]{:T(128)}, s32[]{}) %tuple.42), condition=%wide.region_2.3_spmd.clone, body=%wide.region_1.2_spmd.clone.sunk | while | flops 10244 | bytes 40037 | solution.py:13
  8.9 3.5 gather_fusion
  12.4 3.5 gather_fusion
  16.0 3.5 gather_fusion
  19.6 3.5 gather_fusion
  23.2 3.5 gather_fusion
  26.8 3.5 gather_fusion
  30.4 3.5 gather_fusion
  34.0 3.5 gather_fusion
  37.6 3.5 gather_fusion
  41.1 3.5 gather_fusion
  44.7 2.4 scatter_custom_fusion
  47.2 2.5 scatter_custom_fusion.1
  49.7 9.6 %gather_fusion.2 = bf16[2048,1024]{1,0:T(8,128)(2,1)} fusion(bf16[65,1024]{1,0:T(8,128)(2,1)S(1)} %concatenate.6, s32[2048]{0:T(1024)S(1)} %get-tuple-element.102), kind=kCustom, calls=%fused_computation.2 | custom fusion | bytes 8396800 | tf_op jit(solution)/shard_map/gather | solution.py:72
  59.3 6.7 %all-to-all-start = ((bf16[16,128,1024]{2,1,0:T(8,128)(2,1)}), bf16[16,128,1024]{2,1,0:T(8,128)(2,1)}, u32[]{:S(2)}, u32[]{:S(2)}) async-start(bf16[16,128,1024]{2,1,0:T(8,128)(2,1)} %bitcast.48), calls=%async_computation | async-start | bytes 8388608 | tf_op jit(solution)/shard_map/all_to_all | solution.py:61
  66.0 0.1 copy.17
  66.0 0.1 mul.62
  66.2 0.2 fusion.10
  66.4 0.1 concatenate.7
  66.4 9.6 %gather_fusion.4 = bf16[2048,1024]{1,0:T(8,128)(2,1)} fusion(bf16[513,1024]{1,0:T(8,128)(2,1)S(1)} %concatenate.7, s32[2048]{0:T(1024)S(1)} %get-tuple-element.101), kind=kCustom, calls=%fused_computation.4 | custom fusion | bytes 8396800 | tf_op jit(solution)/shard_map/gather | solution.py:80
  76.1 82.6 %all-to-all-done = bf16[16,128,1024]{2,1,0:T(8,128)(2,1)} async-done(((bf16[16,128,1024]{2,1,0:T(8,128)(2,1)}), bf16[16,128,1024]{2,1,0:T(8,128)(2,1)}, u32[]{:S(2)}, u32[]{:S(2)}) %all-to-all-start) | async-done | bytes 4194336 | tf_op jit(solution)/shard_map/all_to_all | solution.py:61
  158.6 4.9 %all-to-all-start.2 = ((bf16[16,128,1024]{2,1,0:T(8,128)(2,1)}), bf16[16,128,1024]{2,1,0:T(8,128)(2,1)}, u32[]{:S(2)}, u32[]{:S(2)}) async-start(bf16[16,128,1024]{2,1,0:T(8,128)(2,1)} %bitcast.49), calls=%async_computation.2 | async-start | bytes 8388608 | tf_op jit(solution)/shard_map/all_to_all | solution.py:61
  163.6 0.0 slice-start.6
  163.6 2.8 copy.19
  166.4 0.0 copy-start
  166.4 0.0 slice-done
  166.4 0.6 slice-done.1
  167.0 2.4 convolution_convert_fusion.2
  169.4 0.0 copy-done
  169.4 0.4 slice-done.6
  169.8 0.6 slice-done.7
  170.4 2.4 convolution_convert_fusion.1
  172.8 0.1 slice-done.5
  172.9 2.4 convolution_convert_fusion
  175.3 2.5 copy.20
  177.8 78.4 %all-to-all-done.2 = bf16[16,128,1024]{2,1,0:T(8,128)(2,1)} async-done(((bf16[16,128,1024]{2,1,0:T(8,128)(2,1)}), bf16[16,128,1024]{2,1,0:T(8,128)(2,1)}, u32[]{:S(2)}, u32[]{:S(2)}) %all-to-all-start.2) | async-done | bytes 4194336 | tf_op jit(solution)/shard_map/all_to_all | solution.py:61
  256.2 4.8 %all-to-all-start.1 = ((bf16[16,128,1024]{2,1,0:T(8,128)(2,1)}), bf16[16,128,1024]{2,1,0:T(8,128)(2,1)}, u32[]{:S(2)}, u32[]{:S(2)}) async-start(bf16[16,128,1024]{2,1,0:T(8,128)(2,1)} %bitcast.51), calls=%async_computation.1 | async-start | bytes 8388608 | tf_op jit(solution)/shard_map/all_to_all | solution.py:61
  261.0 0.0 copy-start.12
  261.0 0.0 slice-start.2
  261.0 2.8 copy.22
  263.9 0.3 copy-done.12
  264.2 9.1 %fusion.3 = (bf16[8,256,384]{2,1,0:T(8,128)(2,1)S(1)}, f32[8,256,384]{2,1,0:T(8,128)}) fusion(bf16[8,256,384]{2,1,0:T(8,128)(2,1)S(1)} %copy-done.12, bf16[8,256,384]{2,1,0:T(8,128)(2,1)S(1)} %copy-done.9, bf16[8,256,1024]{2,1,0:T(8,128)(2,1)S(1)} %bitcast.60, bf16[8,384,1024]{2,1,0:T(8,128)(2,1)} %param.14), kind=kOutput, calls=%fused_computation.22 | convolution fusion | flops 1620049920 | bytes 18350080 | tf_op jit(solution)/shard_map/ecd,efd->ecf/dot_general | solution.py:41
  273.3 5.8 %fusion.28 = f32[8,256,1024]{2,1,0:T(8,128)} fusion(bf16[8,256,384]{2,1,0:T(8,128)(2,1)S(1)} %get-tuple-element.103, bf16[8,1024,384]{2,1,0:T(8,128)(2,1)S(1)} %bitcast.59), kind=kOutput, calls=%fused_computation.61 | convolution fusion | flops 1610612736 | bytes 16252928 | tf_op jit(solution)/shard_map/ecf,edf->ecd/dot_general | solution.py:49
  279.2 10.5 %add_convert_fusion = bf16[8,256,1024]{2,1,0:T(8,128)(2,1)} fusion(f32[8,256,1024]{2,1,0:T(8,128)} %fusion.28, bf16[8,1024,384]{2,1,0:T(8,128)(2,1)} %param.13, f32[8,256,384]{2,1,0:T(8,128)} %get-tuple-element.104, bf16[8,256,384]{2,1,0:T(8,128)(2,1)S(1)} %copy-done.9), kind=kOutput, calls=%fused_computation.12 | convolution fusion | flops 1620312064 | bytes 23592960 | tf_op jit(solution)/shard_map/ecf,edf->ecd/dot_general | solution.py:49
  289.7 5.0 %copy.23 = bf16[8,16,16,1024]{3,2,0,1:T(8,128)(2,1)} copy(bf16[8,16,16,1024]{3,2,1,0:T(8,128)(2,1)} %bitcast.62) | data formatting | bytes 8388608 | tf_op jit(solution)/shard_map/reshape | solution.py:27
  294.7 59.0 %all-to-all-done.1 = bf16[16,128,1024]{2,1,0:T(8,128)(2,1)} async-done(((bf16[16,128,1024]{2,1,0:T(8,128)(2,1)}), bf16[16,128,1024]{2,1,0:T(8,128)(2,1)}, u32[]{:S(2)}, u32[]{:S(2)}) %all-to-all-start.1) | async-done | bytes 4194336 | tf_op jit(solution)/shard_map/all_to_all | solution.py:61
  353.7 4.8 %all-to-all-start.3 = ((bf16[16,128,1024]{2,1,0:T(8,128)(2,1)}), bf16[16,128,1024]{2,1,0:T(8,128)(2,1)}, u32[]{:S(2)}, u32[]{:S(2)}) async-start(bf16[16,128,1024]{2,1,0:T(8,128)(2,1)} %bitcast.50), calls=%async_computation.3 | async-start | bytes 8388608 | tf_op jit(solution)/shard_map/all_to_all | solution.py:61
  358.5 9.5 %fusion.29 = f32[8,1024,384]{2,1,0:T(8,128)} fusion(bf16[8,256,1024]{2,1,0:T(8,128)(2,1)} %bitcast.54, bf16[8,256,384]{2,1,0:T(8,128)(2,1)S(1)} %get-tuple-element.103), kind=kOutput, calls=%fused_computation.62 | convolution fusion | flops 1610612736 | bytes 18350080 | tf_op jit(solution)/shard_map/ecd,ecf->edf/dot_general | solution.py:47
  368.0 0.0 copy-done.13
  368.1 6.9 %fusion.22 = f32[8,384,1024]{2,1,0:T(8,128)} fusion(bf16[8,256,1024]{2,1,0:T(8,128)(2,1)S(1)} %bitcast.61, bf16[8,256,384]{2,1,0:T(8,128)(2,1)S(1)} %copy-done.13, bf16[8,256,384]{2,1,0:T(8,128)(2,1)S(1)} %copy-done.10), kind=kOutput, calls=%fused_computation.59 | convolution fusion | flops 1616904192 | bytes 19922944 | tf_op jit(solution)/shard_map/ecf,ecd->efd/dot_general | solution.py:40
  375.0 0.0 copy-done.7
  375.0 7.3 %fusion.25 = f32[8,1024,384]{2,1,0:T(8,128)} fusion(bf16[8,256,1024]{2,1,0:T(8,128)(2,1)S(1)} %bitcast.55, f32[8,256,384]{2,1,0:T(8,128)S(1)} %copy-done.7, bf16[8,256,384]{2,1,0:T(8,128)(2,1)S(1)} %copy-done.10), kind=kOutput, calls=%fused_computation.60 | convolution fusion | flops 1616117760 | bytes 21495808 | tf_op jit(solution)/shard_map/ecd,ecf->edf/dot_general | solution.py:48
  382.2 5.5 %gather_fusion.3 = bf16[512,1024]{1,0:T(8,128)(2,1)S(1)} fusion(bf16[2048,1024]{1,0:T(8,128)(2,1)} %bitcast.7, s32[1024]{0:T(1024)S(1)} %pad_clamp_fusion.1), kind=kCustom, calls=%fused_computation.3 | custom fusion | bytes 2099200 | tf_op jit(solution)/shard_map/gather | solution.py:76
  387.7 0.7 fusion.11
  388.4 0.7 copy.28
  389.1 1.3 multiply_reduce_fusion
  390.4 60.7 %all-to-all-done.3 = bf16[16,128,1024]{2,1,0:T(8,128)(2,1)} async-done(((bf16[16,128,1024]{2,1,0:T(8,128)(2,1)}), bf16[16,128,1024]{2,1,0:T(8,128)(2,1)}, u32[]{:S(2)}, u32[]{:S(2)}) %all-to-all-start.3) | async-done | bytes 4194336 | tf_op jit(solution)/shard_map/all_to_all | solution.py:61
  451.1 5.5 %gather_fusion.5 = bf16[512,1024]{1,0:T(8,128)(2,1)S(1)} fusion(bf16[2048,1024]{1,0:T(8,128)(2,1)} %bitcast.17, s32[1024]{0:T(1024)S(1)} %pad_clamp_fusion.1), kind=kCustom, calls=%fused_computation.5 | custom fusion | bytes 2099200 | tf_op jit(solution)/shard_map/gather | solution.py:84
  456.6 1.4 bitcast_reduce_fusion
  (96 shorter events, 0.6 us)
Async XLA Ops:
  8.8 40.9 %copy-start.5 = (bf16[64,1024]{1,0:T(8,128)(2,1)S(1)}, bf16[64,1024]{1,0:T(8,128)(2,1)}, u32[]{:S(2)}) copy-start(bf16[64,1024]{1,0:T(8,128)(2,1)} %param.9) | copy-start | bytes 393220
  59.3 6.7 %copy-start.6 = (f32[64,8]{0,1:T(8,128)S(1)}, f32[64,8]{0,1:T(8,128)}, u32[]{:S(2)}) copy-start(f32[64,8]{0,1:T(8,128)} %param.11) | copy-start | bytes 6148
  59.3 6.8 %copy-start.4 = (bf16[64,1024]{1,0:T(8,128)(2,1)S(1)}, bf16[64,1024]{1,0:T(8,128)(2,1)}, u32[]{:S(2)}) copy-start(bf16[64,1024]{1,0:T(8,128)(2,1)} %param.15) | copy-start | bytes 393220
  59.3 99.3 %all-to-all-start = ((bf16[16,128,1024]{2,1,0:T(8,128)(2,1)}), bf16[16,128,1024]{2,1,0:T(8,128)(2,1)}, u32[]{:S(2)}, u32[]{:S(2)}) async-start(bf16[16,128,1024]{2,1,0:T(8,128)(2,1)} %bitcast.48), calls=%async_computation | async-start | bytes 8388608 | tf_op jit(solution)/shard_map/all_to_all | solution.py:61
  158.6 7.8 %slice-start = ((s8[6291456]{0:T(1024)(128)(4,1)}), s8[2097152]{0:T(1024)(128)(4,1)S(1)}, s32[]{:S(2)}) async-start(s8[6291456]{0:T(1024)(128)(4,1)} %bitcast.56), calls=%async_computation.4 | async-start | bytes 4194304
  158.6 97.6 %all-to-all-start.2 = ((bf16[16,128,1024]{2,1,0:T(8,128)(2,1)}), bf16[16,128,1024]{2,1,0:T(8,128)(2,1)}, u32[]{:S(2)}, u32[]{:S(2)}) async-start(bf16[16,128,1024]{2,1,0:T(8,128)(2,1)} %bitcast.49), calls=%async_computation.2 | async-start | bytes 8388608 | tf_op jit(solution)/shard_map/all_to_all | solution.py:61
  163.6 3.4 slice-start.1
  163.6 6.2 %slice-start.6 = ((s8[6291456]{0:T(1024)(128)(4,1)}), s8[4194304]{0:T(1024)(128)(4,1)S(1)}, s32[]{:S(2)}) async-start(s8[6291456]{0:T(1024)(128)(4,1)} %bitcast.68), calls=%async_computation.10 | async-start | bytes 8388608
  166.4 3.0 copy-start
  167.0 3.4 slice-start.7
  167.0 5.8 %slice-start.4 = ((s8[6291456]{0:T(1024)(128)(4,1)}), s8[4194304]{0:T(1024)(128)(4,1)S(1)}, s32[]{:S(2)}) async-start(s8[6291456]{0:T(1024)(128)(4,1)} %bitcast.66), calls=%async_computation.8 | async-start | bytes 8388608
  170.4 2.4 copy-start.8
  170.4 2.5 slice-start.5
  172.9 2.4 copy-start.11
  256.2 97.5 %all-to-all-start.1 = ((bf16[16,128,1024]{2,1,0:T(8,128)(2,1)}), bf16[16,128,1024]{2,1,0:T(8,128)(2,1)}, u32[]{:S(2)}, u32[]{:S(2)}) async-start(bf16[16,128,1024]{2,1,0:T(8,128)(2,1)} %bitcast.51), calls=%async_computation.1 | async-start | bytes 8388608 | tf_op jit(solution)/shard_map/all_to_all | solution.py:61
  261.0 2.9 copy-start.9
  261.0 3.1 copy-start.12
  261.0 12.3 %slice-start.2 = ((s8[6291456]{0:T(1024)(128)(4,1)}), s8[4194304]{0:T(1024)(128)(4,1)S(1)}, s32[]{:S(2)}) async-start(s8[6291456]{0:T(1024)(128)(4,1)} %bitcast.58), calls=%async_computation.6 | async-start | bytes 8388608
  263.9 9.5 %copy-start.2 = (bf16[8,16,16,1024]{3,2,1,0:T(8,128)(2,1)}, bf16[8,16,16,1024]{3,2,1,0:T(8,128)(2,1)S(1)}, u32[]{:S(2)}) copy-start(bf16[8,16,16,1024]{3,2,1,0:T(8,128)(2,1)S(1)} %copy.22) | copy-start | bytes 12582916
  264.2 9.2 %slice-start.3 = ((s8[6291456]{0:T(1024)(128)(4,1)}), s8[2097152]{0:T(1024)(128)(4,1)S(1)}, s32[]{:S(2)}) async-start(s8[6291456]{0:T(1024)(128)(4,1)} %bitcast.58), calls=%async_computation.7 | async-start | bytes 4194304
  353.7 97.5 %all-to-all-start.3 = ((bf16[16,128,1024]{2,1,0:T(8,128)(2,1)}), bf16[16,128,1024]{2,1,0:T(8,128)(2,1)}, u32[]{:S(2)}, u32[]{:S(2)}) async-start(bf16[16,128,1024]{2,1,0:T(8,128)(2,1)} %bitcast.50), calls=%async_computation.3 | async-start | bytes 8388608 | tf_op jit(solution)/shard_map/all_to_all | solution.py:61
  358.5 9.5 %copy-start.3 = (bf16[8,16,16,1024]{3,2,1,0:T(8,128)(2,1)S(1)}, bf16[8,16,16,1024]{3,2,1,0:T(8,128)(2,1)}, u32[]{:S(2)}) copy-start(bf16[8,16,16,1024]{3,2,1,0:T(8,128)(2,1)} %copy-done.2) | copy-start | bytes 12582916
  358.5 9.5 %copy-start.10 = (bf16[8,256,384]{2,1,0:T(8,128)(2,1)S(1)}, bf16[8,256,384]{2,1,0:T(8,128)(2,1)}, u32[]{:S(2)}) copy-start(bf16[8,256,384]{2,1,0:T(8,128)(2,1)} %copy-done.8) | copy-start | bytes 4718596
  358.5 9.5 %copy-start.13 = (bf16[8,256,384]{2,1,0:T(8,128)(2,1)S(1)}, bf16[8,256,384]{2,1,0:T(8,128)(2,1)}, u32[]{:S(2)}) copy-start(bf16[8,256,384]{2,1,0:T(8,128)(2,1)} %copy-done.11) | copy-start | bytes 4718596
  368.0 6.9 %copy-start.1 = (bf16[8,16,16,1024]{3,2,1,0:T(8,128)(2,1)S(1)}, bf16[8,16,16,1024]{3,2,1,0:T(8,128)(2,1)}, u32[]{:S(2)}) copy-start(bf16[8,16,16,1024]{3,2,1,0:T(8,128)(2,1)} %copy-done) | copy-start | bytes 12582916
  368.1 6.9 %copy-start.7 = (f32[8,256,384]{2,1,0:T(8,128)S(1)}, f32[8,256,384]{2,1,0:T(8,128)}, u32[]{:S(2)}) copy-start(f32[8,256,384]{2,1,0:T(8,128)} %get-tuple-element.104) | copy-start | bytes 9437188
where the time goes:
time: 459 us; the launch traced here: 458 us
  waiting for transfers between devices  281 us (61%)
  local copies, waits for them, and re-layouts  90.3 us (20%)
  matrix products  57.1 us (12%)
  starting transfers between devices  21.2 us (5%)
  other arithmetic  7.11 us (2%)
    all_to_all x4, waiting for transfers between devices, exchange(): return lax.all_to_all(buf, grp, 0, 0, tiled=True)  281 us
    gather x10, local copies, waits for them, and re-layouts, slot_positions(): first = jnp.searchsorted(es, es, side='left').astype(jnp.int32)  34.9 us
    all_to_all x4, starting transfers between devices, exchange(): return lax.all_to_all(buf, grp, 0, 0, tiled=True)  21.2 us
    dot_general x1, matrix products, expert_backward(): jnp.einsum('ecf,edf->ecd', dv, w3, preferred_element_type=jnp.float32)  10.5 us
    gather x1, local copies, waits for them, and re-layouts, local(): dsend = jnp.concatenate([do, zrow])[inv].reshape(nd, el * cap, d)  9.61 us
    gather x1, local copies, waits for them, and re-layouts, local(): send = jnp.concatenate([x, zrow])[inv // top].reshape(nd, el * cap, d)  9.61 us
    dot_general x1, matrix products, expert_backward(): gw1 = jnp.einsum('ecd,ecf->edf', xe, du, preferred_element_type=jnp.float32)  9.51 us
  transfers between devices with their start and end apart: 4, of which 4 were waited for; matrix products, arithmetic and copies ran while one was open for 19% of the time, Pallas kernels for 0%

commit v1 on v0

v1 whole, which is shorter than its diff:
```python
import functools

import jax
import jax.numpy as jnp
from jax import lax
from jax.experimental import pallas as pl
from jax.experimental.pallas import tpu as pltpu
from jax.sharding import PartitionSpec as P

TOK = 64
ND = 16
D = 1024
FF = 384
EL = 8
TOP = 8
CAP = 16
NB = 4
TB = 4 * TOK
RB = 4 * CAP
NT = ND * TOK
BF = jnp.bfloat16
F32 = jnp.float32
VMEM_LIMIT = 67043328


def dot(a, b):
    return lax.dot_general(a, b, (((1,), (0,)), ((), ())), preferred_element_type=F32)


def dot_nt(a, b):
    return lax.dot_general(a, b, (((1,), (1,)), ((), ())), preferred_element_type=F32)


def dot_tn(a, b):
    return lax.dot_general(a, b, (((0,), (0,)), ((), ())), preferred_element_type=F32)


def codes(base, route, gates, code, gate):
    rows = []
    for e in range(EL):
        eq = route == base + e
        rows.append(jnp.sum(jnp.where(eq, 1.0, 0.0), axis=0, keepdims=True))
        gate[e:e + 1, :] = jnp.sum(jnp.where(eq, gates, 0.0), axis=0, keepdims=True)
    mem = jnp.concatenate(rows, axis=0)
    i0 = lax.broadcasted_iota(jnp.int32, (TB, TB), 0)
    i1 = lax.broadcasted_iota(jnp.int32, (TB, TB), 1)
    upper = jnp.where((i0 < i1) & (i0 // TOK == i1 // TOK), 1.0, 0.0).astype(BF)
    src = lax.broadcasted_iota(jnp.int32, (EL, TB), 1) // TOK * CAP
    for b in range(NB):
        m = mem[:, b * TB:(b + 1) * TB]
        rank = dot(m.astype(BF), upper).astype(jnp.int32)
        code[:, b * TB:(b + 1) * TB] = jnp.where(m > 0.5, rank + src, -1)


def select(code, b):
    row = lax.broadcasted_iota(jnp.int32, (RB, TB), 0)
    c = code[:, pl.ds(b * TB, TB)]
    return jnp.concatenate([jnp.broadcast_to(c[e:e + 1], (RB, TB)) == row for e in range(EL)], axis=0)


def spread(gate, b):
    g = gate[:, pl.ds(b * TB, TB)]
    return jnp.concatenate([jnp.broadcast_to(g[e:e + 1], (RB, TB)) for e in range(EL)], axis=0)


def mid_kernel(route, gates, xg, dyg, w1h, w3h, w2h, yp, dxp, dgp, xr, dor, ar, dur, dvr,
               w1, w3, w2, code, gate, wsem, rows, orow, us, vs, gs, ds):
    for e in range(EL):
        pltpu.make_async_copy(w1h.at[e], w1.at[e], wsem.at[e, 0]).start()
        pltpu.make_async_copy(w3h.at[e], w3.at[e], wsem.at[e, 1]).start()
        pltpu.make_async_copy(w2h.at[e], w2.at[e], wsem.at[e, 2]).start()
    base = (lax.axis_index('row') * 4 + lax.axis_index('col')) * EL
    codes(base, route[...], gates[...], code, gate)

    def gather(src, dst):
        def body(b, _):
            p = jnp.where(select(code, b), 1.0, 0.0).astype(BF)
            dst[b] = dot(p, src[pl.ds(b * TB, TB), :]).astype(BF)
            return 0
        lax.fori_loop(0, NB, body, 0)

    def rows_of(ref, e):
        return ref[:, pl.ds(e * RB, RB), :]

    gather(xg, rows)

    def fwd(e, _):
        pltpu.make_async_copy(w1h.at[e], w1.at[e], wsem.at[e, 0]).wait()
        pltpu.make_async_copy(w3h.at[e], w3.at[e], wsem.at[e, 1]).wait()
        pltpu.make_async_copy(w2h.at[e], w2.at[e], wsem.at[e, 2]).wait()
        x = rows_of(rows, e).reshape(NB * RB, D)
        xr[e] = x
        u = dot(x, w1[e]).astype(BF)
        v = dot(x, w3[e]).astype(BF)
        us[e] = u
        vs[e] = v
        uf = u.astype(F32)
        a = (uf * jax.nn.sigmoid(uf) * v.astype(F32)).astype(BF)
        ar[e] = a
        orow[:, pl.ds(e * RB, RB), :] = dot(a, w2[e]).astype(BF).reshape(NB, RB, D)
        return 0

    lax.fori_loop(0, EL, fwd, 0)

    def scatter_y(b, _):
        w = jnp.where(select(code, b), spread(gate, b), 0.0)
        gs[b] = jnp.sum(w, axis=1, keepdims=True)
        hi = w.astype(BF)
        w = w - hi.astype(F32)
        mid = w.astype(BF)
        lo = (w - mid.astype(F32)).astype(BF)
        o = orow[b]
        yp[pl.ds(b * TB, TB), :] = dot_tn(hi, o) + dot_tn(mid, o) + dot_tn(lo, o)
        return 0

    lax.fori_loop(0, NB, scatter_y, 0)
    gather(dyg, rows)

    def bwd(e, _):
        dy = rows_of(rows, e).reshape(NB * RB, D).astype(F32)
        o = rows_of(orow, e).reshape(NB * RB, D).astype(F32)
        ds[:, pl.ds(e * RB, RB), :] = jnp.sum(dy * o, axis=1, keepdims=True).reshape(NB, RB, 1)
        g = gs[:, pl.ds(e * RB, RB), :].reshape(NB * RB, 1)
        do = (g * dy).astype(BF)
        dor[e] = do
        da = dot_nt(do, w2[e])
        u = us[e].astype(F32)
        v = vs[e].astype(F32)
        s = jax.nn.sigmoid(u)
        du = (da * v * s * (1.0 + u * (1.0 - s))).astype(BF)
        dv = (da * u * s).astype(BF)
        dur[e] = du
        dvr[e] = dv
        dx = (dot_nt(du, w1[e]) + dot_nt(dv, w3[e])).astype(BF)
        orow[:, pl.ds(e * RB, RB), :] = dx.reshape(NB, RB, D)
        return 0

    lax.fori_loop(0, EL, bwd, 0)

    def scatter_dx(b, _):
        sel = select(code, b)
        w = jnp.where(sel, 1.0, 0.0)
        dxp[pl.ds(b * TB, TB), :] = dot_tn(w.astype(BF), orow[b])
        dg = w * ds[b]
        for e in range(EL):
            dgp[pl.ds(e, 1), pl.ds(b * TB, TB)] = jnp.sum(dg[e * RB:(e + 1) * RB], axis=0, keepdims=True)
        return 0

    lax.fori_loop(0, NB, scatter_dx, 0)


def mid(route, gates, xg, dyg, w1, w3, w2):
    vm = pl.BlockSpec(memory_space=pltpu.VMEM)
    hb = pl.BlockSpec(memory_space=pl.ANY)
    sds = jax.ShapeDtypeStruct
    R = NB * RB
    return pl.pallas_call(
        mid_kernel,
        out_shape=(sds((NT, D), F32), sds((NT, D), F32), sds((EL, NT), F32),
                   sds((EL, R, D), BF), sds((EL, R, D), BF), sds((EL, R, FF), BF), sds((EL, R, FF), BF), sds((EL, R, FF), BF)),
        in_specs=[vm, vm, vm, vm, hb, hb, hb],
        out_specs=[vm] * 8,
        scratch_shapes=[
            pltpu.VMEM((EL, D, FF), BF), pltpu.VMEM((EL, D, FF), BF), pltpu.VMEM((EL, FF, D), BF),
            pltpu.VMEM((EL, NT), jnp.int32), pltpu.VMEM((EL, NT), F32),
            pltpu.SemaphoreType.DMA((EL, 3)),
            pltpu.VMEM((NB, EL * RB, D), BF), pltpu.VMEM((NB, EL * RB, D), BF),
            pltpu.VMEM((EL, R, FF), BF), pltpu.VMEM((EL, R, FF), BF),
            pltpu.VMEM((NB, EL * RB, 1), F32), pltpu.VMEM((NB, EL * RB, 1), F32),
        ],
        compiler_params=pltpu.CompilerParams(vmem_limit_bytes=VMEM_LIMIT),
        name='mid',
    )(route, gates, xg, dyg, w1, w3, w2)


def dw_kernel(x, do, a, du, dv, g1, g3, g2):
    xb = x[0]
    g1[0] = dot_tn(xb, du[0])
    g3[0] = dot_tn(xb, dv[0])
    g2[0] = dot_tn(a[0], do[0])


def dw(xr, dor, ar, dur, dvr):
    sds = jax.ShapeDtypeStruct
    R = NB * RB
    sp = lambda *s: pl.BlockSpec((1,) + s, lambda e: (e, 0, 0))
    return pl.pallas_call(
        dw_kernel,
        grid=(EL,),
        out_shape=(sds((EL, D, FF), F32), sds((EL, D, FF), F32), sds((EL, FF, D), F32)),
        in_specs=[sp(R, D), sp(R, D), sp(R, FF), sp(R, FF), sp(R, FF)],
        out_specs=[sp(D, FF), sp(D, FF), sp(FF, D)],
        name='dw',
    )(xr, dor, ar, dur, dvr)


def solution(mesh):
    grp = ('row', 'col')
    tspec = P(('dp', 'row', 'col'), None)
    wspec = P(grp, None, None)
    gspec = P(('dp', 'row', 'col'), None, None)

    def local(x, ridx, gates, w1, w3, w2, dy):
        meta = jnp.concatenate([ridx.astype(F32).T, gates.T])
        mg = lax.all_gather(meta, grp, axis=0).transpose(1, 0, 2).reshape(2 * TOP, NT)
        route = mg[:TOP].astype(jnp.int32)
        xg = lax.all_gather(x, grp, axis=0, tiled=True)
        dyg = lax.all_gather(dy, grp, axis=0, tiled=True)
        yp, dxp, dgp, xr, dor, ar, dur, dvr = mid(route, mg[TOP:], xg, dyg, w1, w3, w2)
        y = lax.psum_scatter(yp, grp, scatter_dimension=0, tiled=True).astype(BF)
        dx = lax.psum_scatter(dxp, grp, scatter_dimension=0, tiled=True).astype(BF)
        dgt = lax.all_to_all(dgp.reshape(EL, ND, TOK).transpose(1, 0, 2), grp, 0, 0, tiled=True).reshape(ND * EL, TOK)
        hit = ridx.T[None] == jnp.arange(ND * EL, dtype=jnp.int32)[:, None, None]
        dgates = jnp.sum(jnp.where(hit, dgt[:, None, :], 0.0), axis=0).T
        g1, g3, g2 = dw(xr, dor, ar, dur, dvr)
        return y, dx, dgates, g1, g3, g2

    return jax.shard_map(local, mesh=mesh, in_specs=(tspec, tspec, tspec, wspec, wspec, wspec, tspec),
                         out_specs=(tspec, tspec, tspec, gspec, gspec, gspec), check_vma=False)
```

time: 459 us -> 291 us (0.63)
  the two profiles are of different devices: /device:TPU:13 before, /device:TPU:0 now
where the time goes in v1:
time: 291 us; the launch traced here: 290 us
  waiting for transfers between devices  185 us (64%)
  Pallas kernels  55.3 us (19%)
  blocking collectives  23.6 us (8%)
  between operations  13.8 us (5%)
  other arithmetic  6.21 us (2%)
  starting transfers between devices  3.65 us (1%)
  local copies, waits for them, and re-layouts  3.07 us (1%)
    reduce_scatter x1, waiting for transfers between devices, local(): dx = lax.psum_scatter(dxp, grp, scatter_dimension=0, tiled=True).astype(BF)  74.1 us
    reduce_scatter x1, waiting for transfers between devices, local(): y = lax.psum_scatter(yp, grp, scatter_dimension=0, tiled=True).astype(BF)  46.8 us
    all_gather x1, waiting for transfers between devices, local(): dyg = lax.all_gather(dy, grp, axis=0, tiled=True)  42.4 us
    pallas_call x1, Pallas kernels, mid(): pl.pallas_call(mid_kernel, out_shape=(sds((NT, D), F32), sds((NT, D), F32...  37.7 us
    all_gather x1, blocking collectives, local(): lax.all_gather(meta, grp, axis=0).transpose(1, 0, 2).reshape(2 * TOP, NT)  23.6 us
    all_gather x1, waiting for transfers between devices, local(): xg = lax.all_gather(x, grp, axis=0, tiled=True)  19.5 us
    pallas_call x1, Pallas kernels, dw(): pl.pallas_call(dw_kernel, grid=(EL,), out_shape=(sds((EL, D, FF), F32), s...  17.6 us
  transfers between devices with their start and end apart: 5, of which 4 were waited for; matrix products, arithmetic and copies ran while one was open for 3% of the time, Pallas kernels for 6%

profile of v1, /device:TPU:0, one launch (start us, length us, event | category | flops | bytes accessed | tf_op | source)
XLA Modules:
  0.0 290.4 jit_solution(9390569258863903808)
XLA Ops:
  7.2 0.0 all-gather.4.cloned.1.call-start
  7.2 0.7 all-gather.4.cloned.1.call-update
  7.9 0.0 all-gather.6.cloned.1.call-start
  7.9 0.7 all-gather.6.cloned.1.call-update
  8.6 0.0 reduce-scatter.3.cloned.1.call-start
  8.7 0.7 convert_bitcast_fusion
  9.4 0.7 pad_maximum_fusion
  10.1 23.6 %all-gather = f32[256,64]{1,0:T(8,128)S(1)} all-gather(f32[16,64]{1,0:T(8,128)S(1)} %pad_maximum_fusion), channel_id=2, replica_groups=mesh['dp'=2,'row'=4,'col'=4] {'row','col'}, dimensions={0}, use_global_device_ids=true | all-gather | bytes 69632 | tf_op jit(solution)/shard_map/all_gather | solution.py:205
  33.8 0.7 slice.12.gates
  34.5 0.7 convert_element_type.16.route
  35.2 19.5 %all-gather.4.cloned.1.call-done.xg = bf16[1024,1024]{1,0:T(8,128)(2,1)} async-done(((bf16[64,1024]{1,0:T(8,128)(2,1)}), bf16[1024,1024]{1,0:T(8,128)(2,1)}) %all-gather.4.cloned.1.call-update) | async-done | bytes 2097168 | tf_op jit(solution)/shard_map/all_gather | solution.py:207
  54.7 42.4 %all-gather.6.cloned.1.call-done.dyg = bf16[1024,1024]{1,0:T(8,128)(2,1)} async-done(((bf16[64,1024]{1,0:T(8,128)(2,1)}), bf16[1024,1024]{1,0:T(8,128)(2,1)}) %all-gather.6.cloned.1.call-update) | async-done | bytes 2097168 | tf_op jit(solution)/shard_map/all_gather | solution.py:208
  97.1 37.7 %mid.1 = (f32[1024,1024]{1,0:T(8,128)}, f32[1024,1024]{1,0:T(8,128)}, f32[8,1024]{1,0:T(8,128)}, bf16[8,256,1024]{2,1,0:T(8,128)(2,1)}, bf16[8,256,1024]{2,1,0:T...) custom-call(s32[8,1024]{1,0:T(8,128)} %convert_element_type.16.route, ...), custom_call_target="tpu_custom_call" | custom-call | tf_op jit(solution)/shard_map/mid/pallas_call | solution.py:157
  134.8 0.0 copy-start
  134.8 0.0 reduce-scatter.3.cloned.1.call-update
  134.8 0.0 reduce-scatter.5.cloned.1.call-start
  134.9 0.5 reduce-scatter.5.cloned.1.call-update
  135.4 0.1 copy-done
  135.5 0.1 reshape.21
  135.6 0.7 reshape.23
  136.4 3.5 %all-to-all-start = ((f32[16,1,512]{2,1,0:T(1,128)}), f32[16,1,512]{2,1,0:T(1,128)S(1)}, u32[]{:S(2)}, u32[]{:S(2)}) async-start(f32[16,1,512]{2,1,0:T(1,128)} %reshape.23), calls=%async_computation.2 | async-start | bytes 65536 | tf_op jit(solution)/shard_map/all_to_all | solution.py:212
  139.9 0.0 copy-start.1
  139.9 17.6 %dw.1 = (f32[8,1024,384]{2,1,0:T(8,128)}, f32[8,1024,384]{2,1,0:T(8,128)}, f32[8,384,1024]{2,1,0:T(8,128)}) custom-call(bf16[8,256,1024]{2,1,0:T(8,128)(2,1)} %get-tuple-element.20.x, bf16[8,256,1024]{2,1,0:T(8,128)(2,1)} %get-tuple-element.21.do, bf16[8,256,384]{2,1,0:T(8,128)(2,1)} %get-tuple-element.22.a, bf16[8,256,384]{2,1,0:T(8,128)(2,1)} %get-tuple-element.23.du, ...), custom_call_target="tpu_custom_call" | custom-call | tf_op jit(solution)/shard_map/dw/pallas_call | solution.py:187
  157.5 0.0 all-to-all-done
  157.5 0.5 broadcast.1
  158.0 0.7 reduce
  158.7 0.1 reshape.24
  158.8 0.1 copy.18
  158.9 0.0 copy-done.1
  158.9 0.9 select_reduce_fusion
  159.7 46.8 %reduce-scatter.3.cloned.1.call-done = f32[64,1024]{1,0:T(8,128)} async-done(((f32[1024,1024]{1,0:T(8,128)}), f32[64,1024]{1,0:T(8,128)}) %reduce-scatter.3.cloned.1.call-update) | async-done | bytes 262160 | tf_op jit(solution)/shard_map/reduce_scatter | solution.py:210
  206.5 1.6 convert_element_type.17
  208.1 74.1 %reduce-scatter.5.cloned.1.call-done = f32[64,1024]{1,0:T(8,128)} async-done(((f32[1024,1024]{1,0:T(8,128)}), f32[64,1024]{1,0:T(8,128)}) %reduce-scatter.5.cloned.1.call-update) | async-done | bytes 262160 | tf_op jit(solution)/shard_map/reduce_scatter | solution.py:211
  282.3 1.6 convert_element_type.18
  (3 shorter events, 0.1 us)
Async XLA Ops:
  7.2 47.5 %all-gather.4.cloned.1.call-start = ((), (), s32[]{:S(2)}) async-start(), calls=%async_computation.3 | async-start | bytes 2228224 | tf_op jit(solution)/shard_map/all_gather | solution.py:207
  7.9 89.2 %all-gather.6.cloned.1.call-start = ((), (), s32[]{:S(2)}) async-start(), calls=%async_computation.4 | async-start | bytes 2228224 | tf_op jit(solution)/shard_map/all_gather | solution.py:208
  8.6 197.9 %reduce-scatter.3.cloned.1.call-start = ((), (), s32[]{:S(2)}) async-start(), calls=%async_computation.5 | async-start | bytes 4456448 | tf_op jit(solution)/shard_map/reduce_scatter | solution.py:210
  134.8 0.8 copy-start
  134.8 147.5 %reduce-scatter.5.cloned.1.call-start = ((), (), s32[]{:S(2)}) async-start(), calls=%async_computation.6 | async-start | bytes 4456448 | tf_op jit(solution)/shard_map/reduce_scatter | solution.py:211
  136.4 21.1 %all-to-all-start = ((f32[16,1,512]{2,1,0:T(1,128)}), f32[16,1,512]{2,1,0:T(1,128)S(1)}, u32[]{:S(2)}, u32[]{:S(2)}) async-start(f32[16,1,512]{2,1,0:T(1,128)} %reshape.23), calls=%async_computation.2 | async-start | bytes 65536 | tf_op jit(solution)/shard_map/all_to_all | solution.py:212
  139.9 19.0 %copy-start.1 = (s32[64,8]{0,1:T(8,128)S(1)}, s32[64,8]{0,1:T(8,128)}, u32[]{:S(2)}) copy-start(s32[64,8]{0,1:T(8,128)} %param.8) | copy-start | bytes 6148
Sparse Core Ops, SparseCore 0:
  10.1 44.4 all-gather.3
  56.8 40.2 all-gather.5
  134.9 71.5 reduce-scatter.2
  210.2 72.0 reduce-scatter.4

commit v2 on v1

v2 whole, which is shorter than its diff:
```python
import functools

import jax
import jax.numpy as jnp
from jax import lax
from jax.experimental import pallas as pl
from jax.experimental.pallas import tpu as pltpu
from jax.sharding import PartitionSpec as P

TOK = 64
ND = 16
D = 1024
FF = 384
EL = 8
TOP = 8
CAP = 16
NB = 4
TB = 4 * TOK
RB = 4 * CAP
NT = ND * TOK
BF = jnp.bfloat16
F32 = jnp.float32
VMEM_LIMIT = 67043328


def dot(a, b):
    return lax.dot_general(a, b, (((1,), (0,)), ((), ())), preferred_element_type=F32)


def dot_nt(a, b):
    return lax.dot_general(a, b, (((1,), (1,)), ((), ())), preferred_element_type=F32)


def dot_tn(a, b):
    return lax.dot_general(a, b, (((0,), (0,)), ((), ())), preferred_element_type=F32)


def put_codes(b, base, meta, code, gate):
    m = [meta[NB * b + i] for i in range(NB)]
    route = jnp.concatenate([a[:TOP, :TOK] for a in m], axis=1)
    gates = jnp.concatenate([a[TOP:, :TOK] for a in m], axis=1)
    rows, gr = [], []
    for e in range(EL):
        eq = route == (base + e).astype(F32)
        rows.append(jnp.sum(jnp.where(eq, 1.0, 0.0), axis=0, keepdims=True))
        gr.append(jnp.sum(jnp.where(eq, gates, 0.0), axis=0, keepdims=True))
    mem = jnp.concatenate(rows, axis=0)
    gate[b] = jnp.concatenate(gr, axis=0)
    i0 = lax.broadcasted_iota(jnp.int32, (TB, TB), 0)
    i1 = lax.broadcasted_iota(jnp.int32, (TB, TB), 1)
    upper = jnp.where((i0 < i1) & (i0 // TOK == i1 // TOK), 1.0, 0.0).astype(BF)
    src = lax.broadcasted_iota(jnp.int32, (EL, TB), 1) // TOK * CAP
    rank = dot(mem.astype(BF), upper).astype(jnp.int32)
    code[b] = jnp.where(mem > 0.5, rank + src, -1)


def select(code, b):
    row = lax.broadcasted_iota(jnp.int32, (RB, TB), 0)
    c = code[b]
    return jnp.concatenate([jnp.broadcast_to(c[e:e + 1], (RB, TB)) == row for e in range(EL)], axis=0)


def spread(gate, b):
    g = gate[b]
    return jnp.concatenate([jnp.broadcast_to(g[e:e + 1], (RB, TB)) for e in range(EL)], axis=0)


def place(pos, core):
    y = pos // 4
    return pos + y * (7 - 2 * pos), 2 * y + core


def slot(pos, core):
    row, col = place(pos, core)
    return row * 4 + col


def remote(src, dst, ss, rs, dev):
    return pltpu.make_async_remote_copy(
        src_ref=src, dst_ref=dst, send_sem=ss, recv_sem=rs,
        device_id={'row': dev[0], 'col': dev[1]}, device_id_type=pl.DeviceIdType.MESH)


HALF = TOK // 2


def main_kernel(x, dy, meta, w1h, w3h, w2h, yo, dxo, dgo, xrh, dorh, arh, durh, dvrh,
                w1, w3, w2, wsem, osem, xg, dyg, mg, code, gate, xrow, dyrow, orow, us, vs, av, gs, ds,
                acc, pbuf, rbuf, dgs, dgr,
                ags, agr, pgs, pgr, ms, mr, gss, gsr, rss, rsr, rps, rpr):
    z = lax.axis_index('row')
    c4 = lax.axis_index('col')
    yy = c4 // 2
    core = c4 % 2
    r = z + yy * (7 - 2 * z)
    me = z * 4 + c4
    base = me * EL
    right, left = (r + 1) % 8, (r + 7) % 8
    nbr = (place(right, core), place(left, core))
    partner = (z, 2 * yy + 1 - core)

    def peer(o):
        q = (me + o) % ND
        return q, (q // 4, q % 4)

    barrier = pltpu.get_barrier_semaphore()

    def hello(o, _):
        q, dev = peer(o)
        pl.semaphore_signal(barrier, inc=1, device_id={'row': dev[0], 'col': dev[1]},
                            device_id_type=pl.DeviceIdType.MESH)
        return 0

    lax.fori_loop(1, ND, hello, 0)

    def load(e, _):
        pltpu.make_async_copy(w1h.at[e], w1.at[e], wsem.at[e, 0]).start()
        pltpu.make_async_copy(w3h.at[e], w3.at[e], wsem.at[e, 1]).start()
        pltpu.make_async_copy(w2h.at[e], w2.at[e], wsem.at[e, 2]).start()
        return 0

    lax.fori_loop(0, EL, load, 0)
    xg[me] = x[...]
    dyg[me] = dy[...]
    mg[me] = meta[...]
    pl.semaphore_wait(barrier, ND - 1)

    def meta_copy(o):
        q, dev = peer(o)
        return remote(meta, mg.at[me], ms.at[o], mr.at[o], dev)

    def meta_send(o, _):
        meta_copy(o).start()
        return 0

    def meta_wait(o, _):
        meta_copy(o).wait_recv()
        return 0

    lax.fori_loop(1, ND, meta_send, 0)

    gath = ((x, xg), (dy, dyg))

    def own(t, d, m, src=None):
        h = m if d == 0 else 1 - m
        return remote(gath[t][0].at[pl.ds(h * HALF, HALF)], gath[t][1].at[me, pl.ds(h * HALF, HALF)],
                      ags.at[t, d, m], agr.at[t, d, m], nbr[d])

    def chunk(t, d, m):
        k = 1 + m // 2
        h = m % 2 if d == 0 else 1 - m % 2
        p = slot((r + 8 - k) % 8 if d == 0 else (r + k) % 8, core)
        return gath[t][1].at[p, pl.ds(pl.multiple_of(h * HALF, HALF), HALF)]

    def onward(t, d, m):
        c = chunk(t, d, m)
        return remote(c, c, ags.at[t, d, m + 2], agr.at[t, d, m + 2], nbr[d])

    def across(t, d, m):
        c = chunk(t, d, m)
        return remote(c, c, pgs.at[t, d, m], pgr.at[t, d, m], partner)

    def own_across(t):
        return remote(gath[t][0], gath[t][1].at[me], pgs.at[t, 0, 7], pgr.at[t, 0, 7], partner)

    def ag_start(t):
        for m in range(2):
            for d in range(2):
                own(t, d, m).start()
        own_across(t).start()

    def ag_step(t, m):
        for d in range(2):
            c = chunk(t, d, m)
            remote(c, c, ags.at[t, d, m], agr.at[t, d, m], nbr[d]).wait_recv()

            @pl.when(m <= 4)
            def _():
                onward(t, d, m).start()
            across(t, d, m).start()

    def ag_wait_partner(t):
        def body(m, _):
            for d in range(2):
                across(t, d, m).wait_recv()
            return 0
        lax.fori_loop(0, 7, body, 0)
        own_across(t).wait_recv()

    def ag_drain(t):
        def body(m, _):
            for d in range(2):
                c = chunk(t, d, m)
                remote(c, c, ags.at[t, d, m], agr.at[t, d, m], nbr[d]).wait_send()
                across(t, d, m).wait_send()
            return 0
        lax.fori_loop(0, 7, body, 0)
        own_across(t).wait_send()

    ag_start(0)

    def xstep(m, _):
        ag_step(0, m)

        @pl.when(m == 1)
        def _():
            lax.fori_loop(1, ND, meta_wait, 0)

        @pl.when((m >= 2) & (m < 6))
        def _():
            put_codes(m - 2, base, mg, code, gate)
        return 0

    lax.fori_loop(0, 7, xstep, 0)
    ag_start(1)
    ag_wait_partner(0)

    def gather(src, dst):
        def body(b, _):
            p = jnp.where(select(code, b), 1.0, 0.0).astype(BF)
            dst[b] = dot(p, src[pl.ds(NB * b, NB)].reshape(TB, D)).astype(BF)
            return 0
        lax.fori_loop(0, NB, body, 0)

    def rows_of(ref, e):
        return ref[:, pl.ds(pl.multiple_of(e * RB, RB), RB), :]

    def put_rows(ref, e, v):
        ref[:, pl.ds(pl.multiple_of(e * RB, RB), RB), :] = v.reshape(NB, RB, v.shape[-1])

    gather(xg, xrow)
    out_x = pltpu.make_async_copy(xrow, xrh, osem.at[0])
    out_x.start()

    def fwd(e, _):
        pltpu.make_async_copy(w1h.at[e], w1.at[e], wsem.at[e, 0]).wait()
        pltpu.make_async_copy(w3h.at[e], w3.at[e], wsem.at[e, 1]).wait()
        pltpu.make_async_copy(w2h.at[e], w2.at[e], wsem.at[e, 2]).wait()
        xe = rows_of(xrow, e).reshape(NB * RB, D)
        u = dot(xe, w1[e]).astype(BF)
        v = dot(xe, w3[e]).astype(BF)
        us[e] = u
        vs[e] = v
        uf = u.astype(F32)
        a = (uf * jax.nn.sigmoid(uf) * v.astype(F32)).astype(BF)
        av[e] = a
        put_rows(orow, e, dot(a, w2[e]).astype(BF))

        @pl.when(e < 7)
        def _():
            ag_step(1, e)
        return 0

    lax.fori_loop(0, EL, fwd, 0)
    out_a = pltpu.make_async_copy(av, arh, osem.at[1])
    out_a.start()

    def rs_pair(t, o):
        d = (r + o) % 8
        return remote(acc.at[t, slot(d, 1 - core)], pbuf.at[t, o], rps.at[t, o], rpr.at[t, o], partner)

    def rs_pair_all(t):
        for o in (4, 3, 5, 2, 6, 1, 7, 0):
            rs_pair(t, o).start()

    def rs_join(t, o):
        rs_pair(t, o).wait_recv()
        p = slot((r + o) % 8, core)
        acc[t, p] = acc[t, p] + pbuf[t, o]

    def rs_move(t, d, m):
        dist = 4 - (m + 1) // 2
        h = m % 2 if d == 0 else 1 - m % 2
        p = slot((r + dist) % 8 if d == 0 else (r + 8 - dist) % 8, core)
        rows = pl.ds(pl.multiple_of(h * HALF, HALF), HALF)
        return p, rows, remote(acc.at[t, p, rows], rbuf.at[t, d, m], rss.at[t, d, m], rsr.at[t, d, m], nbr[d])

    def rs_first(t):
        rs_join(t, 4)
        for d in range(2):
            rs_move(t, d, 0)[2].start()
        rs_join(t, 3)
        rs_join(t, 5)
        for d in range(2):
            rs_move(t, d, 1)[2].start()
        for o in (2, 6, 1, 7, 0):
            rs_join(t, o)

    def rs_step(t, m):
        for d in range(2):
            rs_move(t, d, m - 2)[2].wait_recv()
            p, rows, copy = rs_move(t, d, m)
            acc[t, p, rows] = acc[t, p, rows] + rbuf[t, d, m - 2]
            copy.start()

    def rs_last(t, out):
        for m in (5, 6):
            for d in range(2):
                rs_move(t, d, m)[2].wait_recv()
        out[:HALF] = (acc[t, me, :HALF] + rbuf[t, 0, 6] + rbuf[t, 1, 5]).astype(BF)
        out[HALF:] = (acc[t, me, HALF:] + rbuf[t, 0, 5] + rbuf[t, 1, 6]).astype(BF)

    def rs_drain(t):
        def body(m, _):
            for d in range(2):
                rs_move(t, d, m)[2].wait_send()
            return 0
        lax.fori_loop(0, 7, body, 0)

        def pair(o, _):
            rs_pair(t, o).wait_send()
            return 0
        lax.fori_loop(0, 8, pair, 0)

    def scatter_y(b, _):
        w = jnp.where(select(code, b), spread(gate, b), 0.0)
        gs[b] = jnp.sum(w, axis=1, keepdims=True)
        hi = w.astype(BF)
        w = w - hi.astype(F32)
        mid = w.astype(BF)
        lo = (w - mid.astype(F32)).astype(BF)
        o = orow[b]
        acc[0, pl.ds(NB * b, NB)] = (dot_tn(hi, o) + dot_tn(mid, o) + dot_tn(lo, o)).reshape(NB, TOK, D)
        return 0

    lax.fori_loop(0, NB, scatter_y, 0)
    rs_pair_all(0)
    rs_first(0)
    ag_wait_partner(1)
    gather(dyg, dyrow)

    def bwd(e, _):
        dye = rows_of(dyrow, e).reshape(NB * RB, D).astype(F32)
        o = rows_of(orow, e).reshape(NB * RB, D).astype(F32)
        put_rows(ds, e, jnp.sum(dye * o, axis=1, keepdims=True))
        g = rows_of(gs, e).reshape(NB * RB, 1)
        do = (g * dye).astype(BF)
        put_rows(dyrow, e, do)
        da = dot_nt(do, w2[e])
        u = us[e].astype(F32)
        v = vs[e].astype(F32)
        s = jax.nn.sigmoid(u)
        du = (da * v * s * (1.0 + u * (1.0 - s))).astype(BF)
        dv = (da * u * s).astype(BF)
        us[e] = du
        vs[e] = dv
        put_rows(orow, e, (dot_nt(du, w1[e]) + dot_nt(dv, w3[e])).astype(BF))

        @pl.when(e % 2 == 1)
        def _():
            rs_step(0, 2 + e // 2)
        return 0

    lax.fori_loop(0, EL, bwd, 0)
    outs = [pltpu.make_async_copy(dyrow, dorh, osem.at[2]), pltpu.make_async_copy(us, durh, osem.at[3]),
            pltpu.make_async_copy(vs, dvrh, osem.at[4])]
    for c in outs:
        c.start()

    def scatter_dx(b, _):
        w = jnp.where(select(code, b), 1.0, 0.0)
        acc[1, pl.ds(NB * b, NB)] = dot_tn(w.astype(BF), orow[b]).reshape(NB, TOK, D)
        dg = w * ds[b]
        dge = jnp.concatenate([jnp.sum(dg[e * RB:(e + 1) * RB], axis=0, keepdims=True) for e in range(EL)], axis=0)
        for i in range(NB):
            dgs[NB * b + i, :, :TOK] = dge[:, i * TOK:(i + 1) * TOK]
        return 0

    lax.fori_loop(0, NB, scatter_dx, 0)
    rs_step(0, 6)
    rs_pair_all(1)

    def dg_copy(o):
        q, dev = peer(o)
        return remote(dgs.at[q], dgr.at[me], gss.at[o], gsr.at[o], dev)

    def dg_send(o, _):
        dg_copy(o).start()
        return 0

    lax.fori_loop(1, ND, dg_send, 0)
    dgr[me] = dgs[me]
    rs_first(1)
    rs_last(0, yo)

    def dg_wait(o, _):
        dg_copy(o).wait_recv()
        return 0

    lax.fori_loop(1, ND, dg_wait, 0)

    def xrs(m, _):
        rs_step(1, m)
        return 0

    lax.fori_loop(2, 7, xrs, 0)
    ident = lax.broadcasted_iota(jnp.int32, (ND * EL, 128), 0).astype(F32)
    back = dgr[...].reshape(ND * EL, 128)
    for j in range(TOP):
        dgo[j:j + 1] = jnp.sum(jnp.where(ident == meta[j:j + 1], back, 0.0), axis=0, keepdims=True)
    rs_last(1, dxo)

    def small_drain(o, _):
        meta_copy(o).wait_send()
        dg_copy(o).wait_send()
        return 0

    lax.fori_loop(1, ND, small_drain, 0)
    for t in range(2):
        ag_drain(t)
        rs_drain(t)
    out_x.wait()
    out_a.wait()
    for c in outs:
        c.wait()


def main(x, dy, meta, w1, w3, w2):
    vm = pl.BlockSpec(memory_space=pltpu.VMEM)
    hb = pl.BlockSpec(memory_space=pl.ANY)
    sds = jax.ShapeDtypeStruct
    R = NB * RB
    dma = lambda *s: pltpu.SemaphoreType.DMA(s)
    return pl.pallas_call(
        main_kernel,
        out_shape=(sds((TOK, D), BF), sds((TOK, D), BF), sds((TOP, 128), F32),
                   sds((NB, EL * RB, D), BF), sds((NB, EL * RB, D), BF), sds((EL, R, FF), BF), sds((EL, R, FF), BF), sds((EL, R, FF), BF)),
        in_specs=[vm, vm, vm, hb, hb, hb],
        out_specs=[vm, vm, vm] + [hb] * 5,
        scratch_shapes=[
            pltpu.VMEM((EL, D, FF), BF), pltpu.VMEM((EL, D, FF), BF), pltpu.VMEM((EL, FF, D), BF),
            dma(EL, 3), dma(5),
            pltpu.VMEM((ND, TOK, D), BF), pltpu.VMEM((ND, TOK, D), BF), pltpu.VMEM((ND, 2 * TOP, 128), F32),
            pltpu.VMEM((NB, EL, TB), jnp.int32), pltpu.VMEM((NB, EL, TB), F32),
            pltpu.VMEM((NB, EL * RB, D), BF), pltpu.VMEM((NB, EL * RB, D), BF), pltpu.VMEM((NB, EL * RB, D), BF),
            pltpu.VMEM((EL, R, FF), BF), pltpu.VMEM((EL, R, FF), BF), pltpu.VMEM((EL, R, FF), BF),
            pltpu.VMEM((NB, EL * RB, 1), F32), pltpu.VMEM((NB, EL * RB, 1), F32),
            pltpu.VMEM((2, ND, TOK, D), F32), pltpu.VMEM((2, 8, TOK, D), F32), pltpu.VMEM((2, 2, 7, HALF, D), F32),
            pltpu.VMEM((ND, EL, 128), F32), pltpu.VMEM((ND, EL, 128), F32),
            dma(2, 2, 7), dma(2, 2, 7), dma(2, 2, 8), dma(2, 2, 8), dma(ND), dma(ND), dma(ND), dma(ND),
            dma(2, 2, 7), dma(2, 2, 7), dma(2, 8), dma(2, 8),
        ],
        compiler_params=pltpu.CompilerParams(vmem_limit_bytes=VMEM_LIMIT, collective_id=0, has_side_effects=True),
        name='moe',
    )(x, dy, meta, w1, w3, w2)


def dw_kernel(x, do, a, du, dv, g1, g3, g2):
    xb = x[...].reshape(NB * RB, D)
    g1[0] = dot_tn(xb, du[0])
    g3[0] = dot_tn(xb, dv[0])
    g2[0] = dot_tn(a[0], do[...].reshape(NB * RB, D))


def dw(xr, dor, ar, dur, dvr):
    sds = jax.ShapeDtypeStruct
    R = NB * RB
    sp = lambda *s: pl.BlockSpec((1,) + s, lambda e: (e, 0, 0))
    br = pl.BlockSpec((NB, RB, D), lambda e: (0, e, 0))
    return pl.pallas_call(
        dw_kernel,
        grid=(EL,),
        out_shape=(sds((EL, D, FF), F32), sds((EL, D, FF), F32), sds((EL, FF, D), F32)),
        in_specs=[br, br, sp(R, FF), sp(R, FF), sp(R, FF)],
        out_specs=[sp(D, FF), sp(D, FF), sp(FF, D)],
        name='dw',
    )(xr, dor, ar, dur, dvr)


def solution(mesh):
    grp = ('row', 'col')
    tspec = P(('dp', 'row', 'col'), None)
    wspec = P(grp, None, None)
    gspec = P(('dp', 'row', 'col'), None, None)

    def local(x, ridx, gates, w1, w3, w2, dy):
        meta = jnp.pad(jnp.concatenate([ridx.astype(F32), gates], axis=1).T, ((0, 0), (0, 128 - TOK)))
        y, dx, dgt, xr, dor, ar, dur, dvr = main(x, dy, meta, w1, w3, w2)
        g1, g3, g2 = dw(xr, dor, ar, dur, dvr)
        return y, dx, dgt[:, :TOK].T, g1, g3, g2

    return jax.shard_map(local, mesh=mesh, in_specs=(tspec, tspec, tspec, wspec, wspec, wspec, tspec),
                         out_specs=(tspec, tspec, tspec, gspec, gspec, gspec), check_vma=False)
```

time: 291 us -> 115 us (0.40)
  waiting for transfers between devices: 185 us -> 0 us
  Pallas kernels: 55.3 us -> 110 us
  blocking collectives: 23.6 us -> 0 us
  between operations: 13.8 us -> 0.64 us
  other arithmetic: 6.21 us -> 1.38 us
  starting transfers between devices: 3.65 us -> 0 us
    reduce_scatter x2 -> x0, waiting for transfers between devices: 121 us -> none  [the longest x1 74.1 us: local(): dx = lax.psum_scatter(dxp, grp, scatter_dimension=0, tiled=True).astype(BF)]
    all_gather x2 -> x0, waiting for transfers between devices: 61.9 us -> none  [the longest x1 42.4 us: local(): dyg = lax.all_gather(dy, grp, axis=0, tiled=True)]
    pallas_call x1, Pallas kernels: 37.7 us -> 92.1 us  [main(): pl.pallas_call(main_kernel, out_shape=(sds((TOK, D), BF), sds((TOK, D), B...]
    all_gather x1 -> x0, blocking collectives: 23.6 us -> none  [local(): lax.all_gather(meta, grp, axis=0).transpose(1, 0, 2).reshape(2 * TOP, NT)]
    all_to_all x1 -> x0, starting transfers between devices: 3.5 us -> none  [local(): lax.all_to_all(dgp.reshape(EL, ND, TOK).transpose(1, 0, 2), grp, 0, 0, ti...]
  transfers between devices with their start and end apart: 5 -> 0, of which waited for: 4 -> 0; matrix products, arithmetic and copies ran while one was open for 3% -> 0% of each run, Pallas kernels for 6% -> 0%
where the time goes in v2:
time: 115 us
  Pallas kernels  110 us (96%)
  local copies, waits for them, and re-layouts  3.2 us (3%)
  other arithmetic  1.38 us (1%)
    pallas_call x1, Pallas kernels, main(): pl.pallas_call(main_kernel, out_shape=(sds((TOK, D), BF), sds((TOK, D), B...  92.1 us
    pallas_call x1, Pallas kernels, dw(): pl.pallas_call(dw_kernel, grid=(EL,), out_shape=(sds((EL, D, FF), F32), s...  17.6 us

profile of v2, /device:TPU:0, one launch (start us, length us, event | category | flops | bytes accessed | tf_op | source)
XLA Modules:
  0.0 114.9 jit_solution(5956666361858919139)
XLA Ops:
  0.6 0.7 convert_element_type.5
  1.3 0.7 maximum_bitcast_fusion
  2.0 0.6 pad.4.meta
  2.6 92.1 %moe.1 = (bf16[64,1024]{1,0:T(8,128)(2,1)}, bf16[64,1024]{1,0:T(8,128)(2,1)}, f32[8,128]{1,0:T(8,128)}, bf16[4,512,1024]{2,1,0:T(8,128)(2,1)}, bf16[4,512,1024]{...) custom-call(bf16[64,1024]{1,0:T(8,128)(2,1)} %x.3, ...), custom_call_target="tpu_custom_call" | custom-call | tf_op jit(solution)/shard_map/moe/pallas_call | solution.py:424
  94.7 1.3 %slice_bitcast_fusion = f32[64,8]{0,1:T(8,128)} fusion(f32[8,128]{1,0:T(8,128)} %get-tuple-element.19), kind=kLoop, calls=%fused_computation.1 | loop fusion | bytes 4096 | tf_op jit(solution)/shard_map/transpose | solution.py:480
  96.0 0.0 copy-start.1
  96.0 0.0 copy-start
  96.0 17.6 %dw.1 = (f32[8,1024,384]{2,1,0:T(8,128)}, f32[8,1024,384]{2,1,0:T(8,128)}, f32[8,384,1024]{2,1,0:T(8,128)}) custom-call(bf16[4,512,1024]{2,1,0:T(8,128)(2,1)} %get-tuple-element.20.x, bf16[4,512,1024]{2,1,0:T(8,128)(2,1)} %get-tuple-element.21.do, bf16[8,256,384]{2,1,0:T(8,128)(2,1)} %get-tuple-element.22.a, bf16[8,256,384]{2,1,0:T(8,128)(2,1)} %get-tuple-element.23.du, ...), custom_call_target="tpu_custom_call" | custom-call | tf_op jit(solution)/shard_map/dw/pallas_call | solution.py:460
  113.6 0.0 copy-done.1
  113.6 0.7 copy.15
  114.2 0.0 copy-done
  114.2 0.7 copy.16
Async XLA Ops:
  96.0 17.6 %copy-start.1 = (bf16[64,1024]{1,0:T(8,128)(2,1)S(1)}, bf16[64,1024]{1,0:T(8,128)(2,1)}, u32[]{:S(2)}) copy-start(bf16[64,1024]{1,0:T(8,128)(2,1)} %get-tuple-element.34) | copy-start | bytes 393220
  96.0 18.3 %copy-start = (bf16[64,1024]{1,0:T(8,128)(2,1)S(1)}, bf16[64,1024]{1,0:T(8,128)(2,1)}, u32[]{:S(2)}) copy-start(bf16[64,1024]{1,0:T(8,128)(2,1)} %get-tuple-element.35) | copy-start | bytes 393220

commit v3 on v2

--- a/solution.py
+++ b/solution.py
@@ -65,6 +65,20 @@
     return jnp.concatenate([jnp.broadcast_to(g[e:e + 1], (RB, TB)) for e in range(EL)], axis=0)
 
 
+def put_tables(b, code, gate, gs, tab):
+    lane = lax.broadcasted_iota(jnp.int32, (EL, EL * RB), 1)
+    widen = jnp.where(lane // RB == lax.broadcasted_iota(jnp.int32, (EL, EL * RB), 0), 1.0, 0.0).astype(BF)
+    row = (lax.broadcasted_iota(jnp.int32, (TB, EL * RB), 1) % RB).astype(F32)
+    sel = dot_tn(code[b].astype(F32).astype(BF), widen) == row
+    g = gate[b]
+    for i in range(3):
+        part = g.astype(BF)
+        g = g - part.astype(F32)
+        tab[b, i] = jnp.where(sel, dot_tn(part, widen), 0.0).astype(BF)
+    tab[b, 3] = jnp.where(sel, 1.0, 0.0).astype(BF)
+    gs[b] = jnp.sum(jnp.where(select(code, b), spread(gate, b), 0.0), axis=1, keepdims=True)
+
+
 def place(pos, core):
     y = pos // 4
     return pos + y * (7 - 2 * pos), 2 * y + core
@@ -82,10 +96,14 @@
 
 
 HALF = TOK // 2
-
-
-def main_kernel(x, dy, meta, w1h, w3h, w2h, yo, dxo, dgo, xrh, dorh, arh, durh, dvrh,
-                w1, w3, w2, wsem, osem, xg, dyg, mg, code, gate, xrow, dyrow, orow, us, vs, av, gs, ds,
+NC = 4
+CH = TOK // NC
+LAST = 3 * NC + NC // 2
+DH = D // 2
+
+
+def main_kernel(ridx, gates, x, dy, w1h, w3h, w2h, yo, dxo, dgo, xrh, dorh, arh, durh, dvrh,
+                w1, w3, w2, wsem, osem, isem, meta, xg, dyg, mg, code, gate, tab, xrow, orow, us, vs, av, gs, ds,
                 acc, pbuf, rbuf, dgs, dgr,
                 ags, agr, pgs, pgr, ms, mr, gss, gsr, rss, rsr, rps, rpr):
     z = lax.axis_index('row')
@@ -103,6 +121,10 @@
         q = (me + o) % ND
         return q, (q // 4, q % 4)
 
+    in_x = pltpu.make_async_copy(x, xg.at[me], isem.at[0])
+    in_dy = pltpu.make_async_copy(dy, dyg.at[me], isem.at[1])
+    in_x.start()
+    in_dy.start()
     barrier = pltpu.get_barrier_semaphore()
 
     def hello(o, _):
@@ -120,9 +142,12 @@
         return 0
 
     lax.fori_loop(0, EL, load, 0)
-    xg[me] = x[...]
-    dyg[me] = dy[...]
-    mg[me] = meta[...]
+    both = jnp.concatenate([ridx[...].astype(F32), gates[...], jnp.zeros((TOK, 128 - 2 * TOP), F32)], axis=1)
+    turned = jnp.concatenate([both, jnp.zeros((128 - TOK, 128), F32)], axis=0).T
+    meta[...] = turned[:2 * TOP]
+    mg[me] = turned[:2 * TOP]
+    in_x.wait()
+    in_dy.wait()
     pl.semaphore_wait(barrier, ND - 1)
 
     def meta_copy(o):
@@ -139,32 +164,33 @@
 
     lax.fori_loop(1, ND, meta_send, 0)
 
-    gath = ((x, xg), (dy, dyg))
-
-    def own(t, d, m, src=None):
-        h = m if d == 0 else 1 - m
-        return remote(gath[t][0].at[pl.ds(h * HALF, HALF)], gath[t][1].at[me, pl.ds(h * HALF, HALF)],
-                      ags.at[t, d, m], agr.at[t, d, m], nbr[d])
+    gath = (xg, dyg)
+
+    def own(t, d, m):
+        h = m if d == 0 else NC - 1 - m
+        c = gath[t].at[me, pl.ds(h * CH, CH)]
+        return remote(c, c, ags.at[t, d, m], agr.at[t, d, m], nbr[d])
 
     def chunk(t, d, m):
-        k = 1 + m // 2
-        h = m % 2 if d == 0 else 1 - m % 2
+        k = 1 + m // NC
+        h = m % NC if d == 0 else NC - 1 - m % NC
         p = slot((r + 8 - k) % 8 if d == 0 else (r + k) % 8, core)
-        return gath[t][1].at[p, pl.ds(pl.multiple_of(h * HALF, HALF), HALF)]
+        return gath[t].at[p, pl.ds(pl.multiple_of(h * CH, CH), CH)]
 
     def onward(t, d, m):
         c = chunk(t, d, m)
-        return remote(c, c, ags.at[t, d, m + 2], agr.at[t, d, m + 2], nbr[d])
+        return remote(c, c, ags.at[t, d, m + NC], agr.at[t, d, m + NC], nbr[d])
 
     def across(t, d, m):
         c = chunk(t, d, m)
         return remote(c, c, pgs.at[t, d, m], pgr.at[t, d, m], partner)
 
     def own_across(t):
-        return remote(gath[t][0], gath[t][1].at[me], pgs.at[t, 0, 7], pgr.at[t, 0, 7], partner)
+        c = gath[t].at[me]
+        return remote(c, c, pgs.at[t, 0, LAST], pgr.at[t, 0, LAST], partner)
 
     def ag_start(t):
-        for m in range(2):
+        for m in range(NC):
             for d in range(2):
                 own(t, d, m).start()
         own_across(t).start()
@@ -174,7 +200,7 @@
             c = chunk(t, d, m)
             remote(c, c, ags.at[t, d, m], agr.at[t, d, m], nbr[d]).wait_recv()
 
-            @pl.when(m <= 4)
+            @pl.when(m < LAST - NC)
             def _():
                 onward(t, d, m).start()
             across(t, d, m).start()
@@ -184,7 +210,7 @@
             for d in range(2):
                 across(t, d, m).wait_recv()
             return 0
-        lax.fori_loop(0, 7, body, 0)
+        lax.fori_loop(0, LAST, body, 0)
         own_across(t).wait_recv()
 
     def ag_drain(t):
@@ -194,7 +220,7 @@
                 remote(c, c, ags.at[t, d, m], agr.at[t, d, m], nbr[d]).wait_send()
                 across(t, d, m).wait_send()
             return 0
-        lax.fori_loop(0, 7, body, 0)
+        lax.fori_loop(0, LAST, body, 0)
         own_across(t).wait_send()
 
     ag_start(0)
@@ -206,12 +232,16 @@
         def _():
             lax.fori_loop(1, ND, meta_wait, 0)
 
-        @pl.when((m >= 2) & (m < 6))
+        @pl.when((m >= 2) & (m < 10) & (m % 2 == 0))
         def _():
-            put_codes(m - 2, base, mg, code, gate)
-        return 0
-
-    lax.fori_loop(0, 7, xstep, 0)
+            put_codes(m // 2 - 1, base, mg, code, gate)
+
+        @pl.when((m >= 3) & (m < 11) & (m % 2 == 1))
+        def _():
+            put_tables(m // 2 - 1, code, gate, gs, tab)
+        return 0
+
+    lax.fori_loop(0, LAST, xstep, 0)
     ag_start(1)
     ag_wait_partner(0)
 
@@ -235,20 +265,14 @@
     def fwd(e, _):
         pltpu.make_async_copy(w1h.at[e], w1.at[e], wsem.at[e, 0]).wait()
         pltpu.make_async_copy(w3h.at[e], w3.at[e], wsem.at[e, 1]).wait()
-        pltpu.make_async_copy(w2h.at[e], w2.at[e], wsem.at[e, 2]).wait()
         xe = rows_of(xrow, e).reshape(NB * RB, D)
         u = dot(xe, w1[e]).astype(BF)
         v = dot(xe, w3[e]).astype(BF)
         us[e] = u
         vs[e] = v
         uf = u.astype(F32)
-        a = (uf * jax.nn.sigmoid(uf) * v.astype(F32)).astype(BF)
-        av[e] = a
-        put_rows(orow, e, dot(a, w2[e]).astype(BF))
-
-        @pl.when(e < 7)
-        def _():
-            ag_step(1, e)
+        av[e] = (uf * jax.nn.sigmoid(uf) * v.astype(F32)).astype(BF)
+        ag_step(1, e)
         return 0
 
     lax.fori_loop(0, EL, fwd, 0)
@@ -259,9 +283,9 @@
         d = (r + o) % 8
         return remote(acc.at[t, slot(d, 1 - core)], pbuf.at[t, o], rps.at[t, o], rpr.at[t, o], partner)
 
-    def rs_pair_all(t):
-        for o in (4, 3, 5, 2, 6, 1, 7, 0):
-            rs_pair(t, o).start()
+    def rs_pair_block(t, b):
+        for d in (b, 7 - b):
+            rs_pair(t, (d + 8 - r) % 8).start()
 
     def rs_join(t, o):
         rs_pair(t, o).wait_recv()
@@ -294,11 +318,12 @@
             copy.start()
 
     def rs_last(t, out):
+        cols = slice((t % 2) * DH, (t % 2) * DH + DH)
         for m in (5, 6):
             for d in range(2):
                 rs_move(t, d, m)[2].wait_recv()
-        out[:HALF] = (acc[t, me, :HALF] + rbuf[t, 0, 6] + rbuf[t, 1, 5]).astype(BF)
-        out[HALF:] = (acc[t, me, HALF:] + rbuf[t, 0, 5] + rbuf[t, 1, 6]).astype(BF)
+        out[:HALF, cols] = (acc[t, me, :HALF] + rbuf[t, 0, 6] + rbuf[t, 1, 5]).astype(BF)
+        out[HALF:, cols] = (acc[t, me, HALF:] + rbuf[t, 0, 5] + rbuf[t, 1, 6]).astype(BF)
 
     def rs_drain(t):
         def body(m, _):
@@ -312,30 +337,46 @@
             return 0
         lax.fori_loop(0, 8, pair, 0)
 
-    def scatter_y(b, _):
-        w = jnp.where(select(code, b), spread(gate, b), 0.0)
-        gs[b] = jnp.sum(w, axis=1, keepdims=True)
-        hi = w.astype(BF)
-        w = w - hi.astype(F32)
-        mid = w.astype(BF)
-        lo = (w - mid.astype(F32)).astype(BF)
-        o = orow[b]
-        acc[0, pl.ds(NB * b, NB)] = (dot_tn(hi, o) + dot_tn(mid, o) + dot_tn(lo, o)).reshape(NB, TOK, D)
-        return 0
-
-    lax.fori_loop(0, NB, scatter_y, 0)
-    rs_pair_all(0)
-    rs_first(0)
+    def forward_half(c):
+        cols = slice(c * DH, c * DH + DH)
+
+        def out(e, _):
+            if c == 0:
+                pltpu.make_async_copy(w2h.at[e], w2.at[e], wsem.at[e, 2]).wait()
+            orow[:, pl.ds(pl.multiple_of(e * RB, RB), RB), cols] = dot(av[e], w2[e, :, cols]).astype(BF).reshape(NB, RB, DH)
+            return 0
+
+        lax.fori_loop(0, EL, out, 0)
+
+        def scatter(i, _):
+            b = (3 - z + i) % NB
+            o = orow[b, :, cols]
+            acc[c, pl.ds(NB * b, NB)] = (dot(tab[b, 0], o) + dot(tab[b, 1], o) + dot(tab[b, 2], o)).reshape(NB, TOK, DH)
+            rs_pair_block(c, b)
+            if c == 0:
+                @pl.when(i < 3)
+                def _():
+                    ag_step(1, EL + 2 * i)
+                    ag_step(1, EL + 2 * i + 1)
+            return 0
+
+        lax.fori_loop(0, NB, scatter, 0)
+        rs_first(c)
+
+    forward_half(0)
+    forward_half(1)
+    rs_step(0, 2)
     ag_wait_partner(1)
-    gather(dyg, dyrow)
+    out_x.wait()
+    gather(dyg, xrow)
 
     def bwd(e, _):
-        dye = rows_of(dyrow, e).reshape(NB * RB, D).astype(F32)
+        dye = rows_of(xrow, e).reshape(NB * RB, D).astype(F32)
         o = rows_of(orow, e).reshape(NB * RB, D).astype(F32)
         put_rows(ds, e, jnp.sum(dye * o, axis=1, keepdims=True))
         g = rows_of(gs, e).reshape(NB * RB, 1)
         do = (g * dye).astype(BF)
-        put_rows(dyrow, e, do)
+        put_rows(xrow, e, do)
         da = dot_nt(do, w2[e])
         u = us[e].astype(F32)
         v = vs[e].astype(F32)
@@ -346,29 +387,43 @@
         vs[e] = dv
         put_rows(orow, e, (dot_nt(du, w1[e]) + dot_nt(dv, w3[e])).astype(BF))
 
-        @pl.when(e % 2 == 1)
+        @pl.when(e < 7)
         def _():
-            rs_step(0, 2 + e // 2)
+            i = e + 1
+            rs_step((i // 2) % 2, 2 + 2 * (i // 4) + i % 2)
         return 0
 
     lax.fori_loop(0, EL, bwd, 0)
-    outs = [pltpu.make_async_copy(dyrow, dorh, osem.at[2]), pltpu.make_async_copy(us, durh, osem.at[3]),
+    outs = [pltpu.make_async_copy(xrow, dorh, osem.at[2]), pltpu.make_async_copy(us, durh, osem.at[3]),
             pltpu.make_async_copy(vs, dvrh, osem.at[4])]
     for c in outs:
         c.start()
-
-    def scatter_dx(b, _):
-        w = jnp.where(select(code, b), 1.0, 0.0)
-        acc[1, pl.ds(NB * b, NB)] = dot_tn(w.astype(BF), orow[b]).reshape(NB, TOK, D)
-        dg = w * ds[b]
+    rs_step(0, 6)
+
+    def backward_half(c):
+        cols = slice(c * DH, c * DH + DH)
+
+        def scatter(i, _):
+            b = (3 - z + i) % NB
+            acc[2 + c, pl.ds(NB * b, NB)] = dot(tab[b, 3], orow[b, :, cols]).reshape(NB, TOK, DH)
+            rs_pair_block(2 + c, b)
+            return 0
+
+        lax.fori_loop(0, NB, scatter, 0)
+        rs_first(2 + c)
+
+    backward_half(0)
+    rs_step(1, 6)
+    backward_half(1)
+
+    def slots_back(b, _):
+        dg = jnp.where(select(code, b), ds[b], 0.0)
         dge = jnp.concatenate([jnp.sum(dg[e * RB:(e + 1) * RB], axis=0, keepdims=True) for e in range(EL)], axis=0)
         for i in range(NB):
             dgs[NB * b + i, :, :TOK] = dge[:, i * TOK:(i + 1) * TOK]
         return 0
 
-    lax.fori_loop(0, NB, scatter_dx, 0)
-    rs_step(0, 6)
-    rs_pair_all(1)
+    lax.fori_loop(0, NB, slots_back, 0)
 
     def dg_copy(o):
         q, dev = peer(o)
@@ -380,25 +435,30 @@
 
     lax.fori_loop(1, ND, dg_send, 0)
     dgr[me] = dgs[me]
-    rs_first(1)
+    rs_step(2, 2)
+    rs_step(2, 3)
+    rs_step(3, 2)
     rs_last(0, yo)
+    rs_step(3, 3)
+    rs_last(1, yo)
+    rs_step(2, 4)
 
     def dg_wait(o, _):
         dg_copy(o).wait_recv()
         return 0
 
     lax.fori_loop(1, ND, dg_wait, 0)
-
-    def xrs(m, _):
-        rs_step(1, m)
-        return 0
-
-    lax.fori_loop(2, 7, xrs, 0)
-    ident = lax.broadcasted_iota(jnp.int32, (ND * EL, 128), 0).astype(F32)
-    back = dgr[...].reshape(ND * EL, 128)
-    for j in range(TOP):
-        dgo[j:j + 1] = jnp.sum(jnp.where(ident == meta[j:j + 1], back, 0.0), axis=0, keepdims=True)
-    rs_last(1, dxo)
+    rs_step(2, 5)
+    expert = lax.broadcasted_iota(jnp.int32, (TOK, ND * EL), 1)
+    back = dgr[...].reshape(ND * EL, 128).T[:TOK]
+    dgo[...] = jnp.concatenate(
+        [jnp.sum(jnp.where(expert == ridx[:, j:j + 1], back, 0.0), axis=1, keepdims=True) for j in range(TOP)], axis=1)
+    rs_step(3, 4)
+    rs_step(3, 5)
+    rs_step(2, 6)
+    rs_step(3, 6)
+    rs_last(2, dxo)
+    rs_last(3, dxo)
 
     def small_drain(o, _):
         meta_copy(o).wait_send()
@@ -408,14 +468,14 @@
     lax.fori_loop(1, ND, small_drain, 0)
     for t in range(2):
         ag_drain(t)
+    for t in range(4):
         rs_drain(t)
-    out_x.wait()
     out_a.wait()
     for c in outs:
         c.wait()
 
 
-def main(x, dy, meta, w1, w3, w2):
+def main(ridx, gates, x, dy, w1, w3, w2):
     vm = pl.BlockSpec(memory_space=pltpu.VMEM)
     hb = pl.BlockSpec(memory_space=pl.ANY)
     sds = jax.ShapeDtypeStruct
@@ -423,48 +483,57 @@
     dma = lambda *s: pltpu.SemaphoreType.DMA(s)
     return pl.pallas_call(
         main_kernel,
-        out_shape=(sds((TOK, D), BF), sds((TOK, D), BF), sds((TOP, 128), F32),
+        out_shape=(sds((TOK, D), BF), sds((TOK, D), BF), sds((TOK, TOP), F32),
                    sds((NB, EL * RB, D), BF), sds((NB, EL * RB, D), BF), sds((EL, R, FF), BF), sds((EL, R, FF), BF), sds((EL, R, FF), BF)),
-        in_specs=[vm, vm, vm, hb, hb, hb],
+        in_specs=[vm, vm, hb, hb, hb, hb, hb],
         out_specs=[vm, vm, vm] + [hb] * 5,
         scratch_shapes=[
             pltpu.VMEM((EL, D, FF), BF), pltpu.VMEM((EL, D, FF), BF), pltpu.VMEM((EL, FF, D), BF),
-            dma(EL, 3), dma(5),
+            dma(EL, 3), dma(5), dma(2), pltpu.VMEM((2 * TOP, 128), F32),
             pltpu.VMEM((ND, TOK, D), BF), pltpu.VMEM((ND, TOK, D), BF), pltpu.VMEM((ND, 2 * TOP, 128), F32),
-            pltpu.VMEM((NB, EL, TB), jnp.int32), pltpu.VMEM((NB, EL, TB), F32),
-            pltpu.VMEM((NB, EL * RB, D), BF), pltpu.VMEM((NB, EL * RB, D), BF), pltpu.VMEM((NB, EL * RB, D), BF),
+            pltpu.VMEM((NB, EL, TB), jnp.int32), pltpu.VMEM((NB, EL, TB), F32), pltpu.VMEM((NB, 4, TB, EL * RB), BF),
+            pltpu.VMEM((NB, EL * RB, D), BF), pltpu.VMEM((NB, EL * RB, D), BF),
             pltpu.VMEM((EL, R, FF), BF), pltpu.VMEM((EL, R, FF), BF), pltpu.VMEM((EL, R, FF), BF),
             pltpu.VMEM((NB, EL * RB, 1), F32), pltpu.VMEM((NB, EL * RB, 1), F32),
-            pltpu.VMEM((2, ND, TOK, D), F32), pltpu.VMEM((2, 8, TOK, D), F32), pltpu.VMEM((2, 2, 7, HALF, D), F32),
+            pltpu.VMEM((4, ND, TOK, DH), F32), pltpu.VMEM((4, 8, TOK, DH), F32), pltpu.VMEM((4, 2, 7, HALF, DH), F32),
             pltpu.VMEM((ND, EL, 128), F32), pltpu.VMEM((ND, EL, 128), F32),
-            dma(2, 2, 7), dma(2, 2, 7), dma(2, 2, 8), dma(2, 2, 8), dma(ND), dma(ND), dma(ND), dma(ND),
-            dma(2, 2, 7), dma(2, 2, 7), dma(2, 8), dma(2, 8),
+            dma(2, 2, LAST), dma(2, 2, LAST), dma(2, 2, LAST + 1), dma(2, 2, LAST + 1), dma(ND), dma(ND), dma(ND), dma(ND),
+            dma(4, 2, 7), dma(4, 2, 7), dma(4, 8), dma(4, 8),
         ],
         compiler_params=pltpu.CompilerParams(vmem_limit_bytes=VMEM_LIMIT, collective_id=0, has_side_effects=True),
         name='moe',
-    )(x, dy, meta, w1, w3, w2)
-
-
-def dw_kernel(x, do, a, du, dv, g1, g3, g2):
-    xb = x[...].reshape(NB * RB, D)
+    )(ridx, gates, x, dy, w1, w3, w2)
+
+
+def dw_kernel(y, dx, dg, x, do, a, du, dv, yo, dxo, dgo, g1, g3, g2):
+    @pl.when((pl.program_id(0) == 0) & (pl.program_id(1) == 0))
+    def _():
+        yo[...] = y[...]
+        dxo[...] = dx[...]
+        dgo[...] = dg[...]
+    xb = x[...].reshape(NB * RB, DH)
     g1[0] = dot_tn(xb, du[0])
     g3[0] = dot_tn(xb, dv[0])
-    g2[0] = dot_tn(a[0], do[...].reshape(NB * RB, D))
-
-
-def dw(xr, dor, ar, dur, dvr):
+    g2[0] = dot_tn(a[0], do[...].reshape(NB * RB, DH))
+
+
+def dw(y, dx, dg, xr, dor, ar, dur, dvr):
     sds = jax.ShapeDtypeStruct
     R = NB * RB
-    sp = lambda *s: pl.BlockSpec((1,) + s, lambda e: (e, 0, 0))
-    br = pl.BlockSpec((NB, RB, D), lambda e: (0, e, 0))
+    whole = lambda *s: pl.BlockSpec(s, lambda e, h: (0, 0))
+    act = pl.BlockSpec((1, R, FF), lambda e, h: (e, 0, 0))
+    br = pl.BlockSpec((NB, RB, DH), lambda e, h: (0, e, h))
+    same = [whole(TOK, D), whole(TOK, D), whole(TOK, TOP)]
     return pl.pallas_call(
         dw_kernel,
-        grid=(EL,),
-        out_shape=(sds((EL, D, FF), F32), sds((EL, D, FF), F32), sds((EL, FF, D), F32)),
-        in_specs=[br, br, sp(R, FF), sp(R, FF), sp(R, FF)],
-        out_specs=[sp(D, FF), sp(D, FF), sp(FF, D)],
+        grid=(EL, 2),
+        out_shape=(sds((TOK, D), BF), sds((TOK, D), BF), sds((TOK, TOP), F32),
+                   sds((EL, D, FF), F32), sds((EL, D, FF), F32), sds((EL, FF, D), F32)),
+        in_specs=same + [br, br, act, act, act],
+        out_specs=same + [pl.BlockSpec((1, DH, FF), lambda e, h: (e, h, 0)), pl.BlockSpec((1, DH, FF), lambda e, h: (e, h, 0)),
+                          pl.BlockSpec((1, FF, DH), lambda e, h: (e, 0, h))],
         name='dw',
-    )(xr, dor, ar, dur, dvr)
+    )(y, dx, dg, xr, dor, ar, dur, dvr)
 
 
 def solution(mesh):
@@ -474,10 +543,7 @@
     gspec = P(('dp', 'row', 'col'), None, None)
 
     def local(x, ridx, gates, w1, w3, w2, dy):
-        meta = jnp.pad(jnp.concatenate([ridx.astype(F32), gates], axis=1).T, ((0, 0), (0, 128 - TOK)))
-        y, dx, dgt, xr, dor, ar, dur, dvr = main(x, dy, meta, w1, w3, w2)
-        g1, g3, g2 = dw(xr, dor, ar, dur, dvr)
-        return y, dx, dgt[:, :TOK].T, g1, g3, g2
+        return dw(*main(ridx, gates, x, dy, w1, w3, w2))
 
     return jax.shard_map(local, mesh=mesh, in_specs=(tspec, tspec, tspec, wspec, wspec, wspec, tspec),
                          out_specs=(tspec, tspec, tspec, gspec, gspec, gspec), check_vma=False)

time: 115 us -> 119 us (1.035)
  Pallas kernels: 110 us -> 113 us
  other arithmetic: 1.38 us -> 0 us
    pallas_call x1, Pallas kernels: 17.6 us -> 22.7 us  [dw(): pl.pallas_call(dw_kernel, grid=(EL, 2), out_shape=(sds((TOK, D), BF), sds...]
    pallas_call x1, Pallas kernels: 92.1 us -> 90.6 us  [main(): pl.pallas_call(main_kernel, out_shape=(sds((TOK, D), BF), sds((TOK, D), B...]
    unnamed x6 -> x2, local copies, waits for them, and re-layouts: 1.32 us -> 2.77 us
    pallas_call x0 -> x1, local copies, waits for them, and re-layouts: none -> 1.42 us  [dw(): pl.pallas_call(dw_kernel, grid=(EL, 2), out_shape=(sds((TOK, D), BF), sds...]
    transpose x1 -> x0, local copies, waits for them, and re-layouts: 1.28 us -> none  [local(): return (y, dx, dgt[:, :TOK].T, g1, g3, g2)]
where the time goes in v3:
time: 119 us; the launch traced here: 118 us
  Pallas kernels  113 us (95%)
  local copies, waits for them, and re-layouts  4.19 us (4%)
    pallas_call x1, Pallas kernels, main(): pl.pallas_call(main_kernel, out_shape=(sds((TOK, D), BF), sds((TOK, D), B...  90.6 us
    pallas_call x1, Pallas kernels, dw(): pl.pallas_call(dw_kernel, grid=(EL, 2), out_shape=(sds((TOK, D), BF), sds...  22.7 us
    unnamed x2, local copies, waits for them, and re-layouts  2.77 us

profile of v3, /device:TPU:0, one launch (start us, length us, event | category | flops | bytes accessed | tf_op | source)
XLA Modules:
  0.0 118.1 jit_solution(6534213257586723190)
XLA Ops:
  0.6 1.4 %copy.13.ridx = s32[64,8]{1,0:T(8,128)} copy(s32[64,8]{0,1:T(8,128)} %param.8) | data formatting | bytes 4096 | tf_op args[1]
  2.0 1.4 %copy.14.gates = f32[64,8]{1,0:T(8,128)} copy(f32[64,8]{0,1:T(8,128)} %param.9) | data formatting | bytes 4096 | tf_op args[2]
  3.4 90.6 %moe.1 = (bf16[64,1024]{1,0:T(8,128)(2,1)}, bf16[64,1024]{1,0:T(8,128)(2,1)}, f32[64,8]{1,0:T(8,128)}, bf16[4,512,1024]{2,1,0:T(8,128)(2,1)}, bf16[4,512,1024]{2...) custom-call(s32[64,8]{1,0:T(8,128)} %copy.13.ridx, ...), custom_call_target="tpu_custom_call" | custom-call | tf_op jit(solution)/shard_map/moe/pallas_call | solution.py:484
  94.0 22.7 %dw.1 = (bf16[64,1024]{1,0:T(8,128)(2,1)}, bf16[64,1024]{1,0:T(8,128)(2,1)}, f32[64,8]{1,0:T(8,128)}, f32[8,1024,384]{2,1,0:T(8,128)}, f32[8,1024,384]{2,1,0:T(8,128)}, /*index=5*/f32[8,384,1024]{2,1,0:T(8,128)}) custom-call(bf16[64,1024]{1,0:T(8,128)(2,1)} %get-tuple-element.14.y, bf16[64,1024]{1,0:T(8,128)(2,1)} %get-tuple-element.15.dx, ...), custom_call_target="tpu_custom_call" | custom-call | tf_op jit(solution)/shard_map/dw/pallas_call | solution.py:527
  116.7 1.4 %copy.15 = f32[64,8]{0,1:T(8,128)} copy(f32[64,8]{1,0:T(8,128)} %get-tuple-element.24) | data formatting | bytes 4096 | tf_op jit(solution)/shard_map/dw/pallas_call | solution.py:527

commit v4 on v3

--- a/solution.py
+++ b/solution.py
@@ -142,10 +142,10 @@
         return 0
 
     lax.fori_loop(0, EL, load, 0)
-    both = jnp.concatenate([ridx[...].astype(F32), gates[...], jnp.zeros((TOK, 128 - 2 * TOP), F32)], axis=1)
-    turned = jnp.concatenate([both, jnp.zeros((128 - TOK, 128), F32)], axis=0).T
-    meta[...] = turned[:2 * TOP]
-    mg[me] = turned[:2 * TOP]
+    both = jnp.concatenate([ridx[...].astype(F32), gates[...]], axis=0)
+    both = jnp.concatenate([both, jnp.zeros((2 * TOP, 128 - TOK), F32)], axis=1)
+    meta[...] = both
+    mg[me] = both
     in_x.wait()
     in_dy.wait()
     pl.semaphore_wait(barrier, ND - 1)
@@ -449,10 +449,10 @@
 
     lax.fori_loop(1, ND, dg_wait, 0)
     rs_step(2, 5)
-    expert = lax.broadcasted_iota(jnp.int32, (TOK, ND * EL), 1)
-    back = dgr[...].reshape(ND * EL, 128).T[:TOK]
+    expert = lax.broadcasted_iota(jnp.int32, (ND * EL, TOK), 0)
+    back = dgr[...].reshape(ND * EL, 128)[:, :TOK]
     dgo[...] = jnp.concatenate(
-        [jnp.sum(jnp.where(expert == ridx[:, j:j + 1], back, 0.0), axis=1, keepdims=True) for j in range(TOP)], axis=1)
+        [jnp.sum(jnp.where(expert == ridx[j:j + 1], back, 0.0), axis=0, keepdims=True) for j in range(TOP)], axis=0)
     rs_step(3, 4)
     rs_step(3, 5)
     rs_step(2, 6)
@@ -483,7 +483,7 @@
     dma = lambda *s: pltpu.SemaphoreType.DMA(s)
     return pl.pallas_call(
         main_kernel,
-        out_shape=(sds((TOK, D), BF), sds((TOK, D), BF), sds((TOK, TOP), F32),
+        out_shape=(sds((TOK, D), BF), sds((TOK, D), BF), sds((TOP, TOK), F32),
                    sds((NB, EL * RB, D), BF), sds((NB, EL * RB, D), BF), sds((EL, R, FF), BF), sds((EL, R, FF), BF), sds((EL, R, FF), BF)),
         in_specs=[vm, vm, hb, hb, hb, hb, hb],
         out_specs=[vm, vm, vm] + [hb] * 5,
@@ -506,32 +506,32 @@
 
 
 def dw_kernel(y, dx, dg, x, do, a, du, dv, yo, dxo, dgo, g1, g3, g2):
-    @pl.when((pl.program_id(0) == 0) & (pl.program_id(1) == 0))
+    @pl.when(pl.program_id(0) == 0)
     def _():
         yo[...] = y[...]
         dxo[...] = dx[...]
         dgo[...] = dg[...]
-    xb = x[...].reshape(NB * RB, DH)
+    xb = x[...].reshape(NB * RB, D)
     g1[0] = dot_tn(xb, du[0])
     g3[0] = dot_tn(xb, dv[0])
-    g2[0] = dot_tn(a[0], do[...].reshape(NB * RB, DH))
+    g2[0] = dot_tn(a[0], do[...].reshape(NB * RB, D))
 
 
 def dw(y, dx, dg, xr, dor, ar, dur, dvr):
     sds = jax.ShapeDtypeStruct
     R = NB * RB
-    whole = lambda *s: pl.BlockSpec(s, lambda e, h: (0, 0))
-    act = pl.BlockSpec((1, R, FF), lambda e, h: (e, 0, 0))
-    br = pl.BlockSpec((NB, RB, DH), lambda e, h: (0, e, h))
-    same = [whole(TOK, D), whole(TOK, D), whole(TOK, TOP)]
+    whole = lambda *s: pl.BlockSpec(s, lambda e: (0, 0))
+    act = pl.BlockSpec((1, R, FF), lambda e: (e, 0, 0))
+    br = pl.BlockSpec((NB, RB, D), lambda e: (0, e, 0))
+    same = [whole(TOK, D), whole(TOK, D), whole(TOP, TOK)]
     return pl.pallas_call(
         dw_kernel,
-        grid=(EL, 2),
-        out_shape=(sds((TOK, D), BF), sds((TOK, D), BF), sds((TOK, TOP), F32),
+        grid=(EL,),
+        out_shape=(sds((TOK, D), BF), sds((TOK, D), BF), sds((TOP, TOK), F32),
                    sds((EL, D, FF), F32), sds((EL, D, FF), F32), sds((EL, FF, D), F32)),
         in_specs=same + [br, br, act, act, act],
-        out_specs=same + [pl.BlockSpec((1, DH, FF), lambda e, h: (e, h, 0)), pl.BlockSpec((1, DH, FF), lambda e, h: (e, h, 0)),
-                          pl.BlockSpec((1, FF, DH), lambda e, h: (e, 0, h))],
+        out_specs=same + [pl.BlockSpec((1, D, FF), lambda e: (e, 0, 0)), pl.BlockSpec((1, D, FF), lambda e: (e, 0, 0)),
+                          pl.BlockSpec((1, FF, D), lambda e: (e, 0, 0))],
         name='dw',
     )(y, dx, dg, xr, dor, ar, dur, dvr)
 
@@ -543,7 +543,8 @@
     gspec = P(('dp', 'row', 'col'), None, None)
 
     def local(x, ridx, gates, w1, w3, w2, dy):
-        return dw(*main(ridx, gates, x, dy, w1, w3, w2))
+        y, dx, dg, g1, g3, g2 = dw(*main(ridx.T, gates.T, x, dy, w1, w3, w2))
+        return y, dx, dg.T, g1, g3, g2
 
     return jax.shard_map(local, mesh=mesh, in_specs=(tspec, tspec, tspec, wspec, wspec, wspec, tspec),
                          out_specs=(tspec, tspec, tspec, gspec, gspec, gspec), check_vma=False)

time: 119 us -> 110 us (0.924)
  Pallas kernels: 113 us -> 108 us
  local copies, waits for them, and re-layouts: 4.19 us -> 0 us
    pallas_call x1, Pallas kernels: 22.7 us -> 17.9 us  [dw(): pl.pallas_call(dw_kernel, grid=(EL,), out_shape=(sds((TOK, D), BF), sds((...]
    unnamed x2 -> x0, local copies, waits for them, and re-layouts: 2.77 us -> none
    pallas_call x1 -> x0, local copies, waits for them, and re-layouts: 1.42 us -> none  [dw(): pl.pallas_call(dw_kernel, grid=(EL, 2), out_shape=(sds((TOK, D), BF), sds...]
where the time goes in v4:
time: 110 us; the launch traced here: 109 us
  Pallas kernels  108 us (98%)
    pallas_call x1, Pallas kernels, main(): pl.pallas_call(main_kernel, out_shape=(sds((TOK, D), BF), sds((TOK, D), B...  90.6 us
    pallas_call x1, Pallas kernels, dw(): pl.pallas_call(dw_kernel, grid=(EL,), out_shape=(sds((TOK, D), BF), sds((...  17.9 us

profile of v4, /device:TPU:0, one launch (start us, length us, event | category | flops | bytes accessed | tf_op | source)
XLA Modules:
  0.0 109.1 jit_solution(14266880297522483249)
XLA Ops:
  0.6 90.6 %moe.1 = (bf16[64,1024]{1,0:T(8,128)(2,1)}, bf16[64,1024]{1,0:T(8,128)(2,1)}, f32[8,64]{1,0:T(8,128)}, bf16[4,512,1024]{2,1,0:T(8,128)(2,1)}, bf16[4,512,1024]{2...) custom-call(s32[8,64]{1,0:T(8,128)} %bitcast.3, ...), custom_call_target="tpu_custom_call" | custom-call | tf_op jit(solution)/shard_map/moe/pallas_call | solution.py:484
  91.2 17.9 %dw.1 = (bf16[64,1024]{1,0:T(8,128)(2,1)}, bf16[64,1024]{1,0:T(8,128)(2,1)}, f32[8,64]{1,0:T(8,128)}, f32[8,1024,384]{2,1,0:T(8,128)}, f32[8,1024,384]{2,1,0:T(8,128)}, /*index=5*/f32[8,384,1024]{2,1,0:T(8,128)}) custom-call(bf16[64,1024]{1,0:T(8,128)(2,1)} %get-tuple-element.20.y, bf16[64,1024]{1,0:T(8,128)(2,1)} %get-tuple-element.21.dx, ...), custom_call_target="tpu_custom_call" | custom-call | tf_op jit(solution)/shard_map/dw/pallas_call | solution.py:527

commit v5 on v4

v5 whole, which is shorter than its diff:
```python
import functools

import jax
import jax.numpy as jnp
from jax import lax
from jax.experimental import pallas as pl
from jax.experimental.pallas import tpu as pltpu
from jax.sharding import PartitionSpec as P

TOK = 64
ND = 16
D = 1024
FF = 384
EL = 8
TOP = 8
CAP = 16
NB = 4
TB = 4 * TOK
RB = 4 * CAP
NT = ND * TOK
BF = jnp.bfloat16
F32 = jnp.float32
VMEM_LIMIT = 67043328


def dot(a, b):
    return lax.dot_general(a, b, (((1,), (0,)), ((), ())), preferred_element_type=F32)


def dot_nt(a, b):
    return lax.dot_general(a, b, (((1,), (1,)), ((), ())), preferred_element_type=F32)


def dot_tn(a, b):
    return lax.dot_general(a, b, (((0,), (0,)), ((), ())), preferred_element_type=F32)


def put_codes(b, base, meta, code, gate):
    m = [meta[NB * b + i] for i in range(NB)]
    route = jnp.concatenate([a[:, :TOK] for a in m], axis=1)
    gates = jnp.concatenate([a[:, TOK:] for a in m], axis=1)
    rows, gr = [], []
    for e in range(EL):
        eq = route == (base + e).astype(F32)
        rows.append(jnp.sum(jnp.where(eq, 1.0, 0.0), axis=0, keepdims=True))
        gr.append(jnp.sum(jnp.where(eq, gates, 0.0), axis=0, keepdims=True))
    mem = jnp.concatenate(rows, axis=0)
    gate[b] = jnp.concatenate(gr, axis=0)
    i0 = lax.broadcasted_iota(jnp.int32, (TB, TB), 0)
    i1 = lax.broadcasted_iota(jnp.int32, (TB, TB), 1)
    upper = jnp.where((i0 < i1) & (i0 // TOK == i1 // TOK), 1.0, 0.0).astype(BF)
    src = lax.broadcasted_iota(jnp.int32, (EL, TB), 1) // TOK * CAP
    rank = dot(mem.astype(BF), upper).astype(jnp.int32)
    code[b] = jnp.where(mem > 0.5, rank + src, -1)


def select(code, b):
    row = lax.broadcasted_iota(jnp.int32, (RB, TB), 0)
    c = code[b]
    return jnp.concatenate([jnp.broadcast_to(c[e:e + 1], (RB, TB)) == row for e in range(EL)], axis=0)


def spread(gate, b):
    g = gate[b]
    return jnp.concatenate([jnp.broadcast_to(g[e:e + 1], (RB, TB)) for e in range(EL)], axis=0)


def put_tables(b, code, gate, gs, tab):
    lane = lax.broadcasted_iota(jnp.int32, (EL, EL * RB), 1)
    widen = jnp.where(lane // RB == lax.broadcasted_iota(jnp.int32, (EL, EL * RB), 0), 1.0, 0.0).astype(BF)
    row = (lax.broadcasted_iota(jnp.int32, (TB, EL * RB), 1) % RB).astype(F32)
    sel = dot_tn(code[b].astype(F32).astype(BF), widen) == row
    g = gate[b]
    for i in range(3):
        part = g.astype(BF)
        g = g - part.astype(F32)
        tab[b, i] = jnp.where(sel, dot_tn(part, widen), 0.0).astype(BF)
    tab[b, 3] = jnp.where(sel, 1.0, 0.0).astype(BF)
    gs[b] = jnp.sum(jnp.where(select(code, b), spread(gate, b), 0.0), axis=1, keepdims=True)


def place(pos, core):
    y = pos // 4
    return pos + y * (7 - 2 * pos), 2 * y + core


def remote(src, dst, ss, rs, dev):
    return pltpu.make_async_remote_copy(
        src_ref=src, dst_ref=dst, send_sem=ss, recv_sem=rs,
        device_id={'row': dev[0], 'col': dev[1]}, device_id_type=pl.DeviceIdType.MESH)


HALF = TOK // 2
NC = 4
CH = TOK // NC
LAST = 3 * NC + NC // 2
DH = D // 2
PEERS = [(o, k) for o in range(8) for k in range(2)][1:]


def main_kernel(ridx, gates, x, dy, w1h, w3h, w2h, yo, dxo, dgo, xrh, dorh, arh, durh, dvrh,
                w1, w3, w2, wsem, osem, isem, meta, xg, dyg, mg, code, gate, tab, xrow, orow, us, vs, av, gs, ds,
                acc, pbuf, rbuf, dgs, dgr,
                ags, agr, pgs, pgr, ms, mr, gss, gsr, rss, rsr, rps, rpr):
    z = lax.axis_index('row')
    c4 = lax.axis_index('col')
    yy = c4 // 2
    core = c4 % 2
    r = z + yy * (7 - 2 * z)
    base = (z * 4 + c4) * EL
    nbr = (place((r + 1) % 8, core), place((r + 7) % 8, core))
    partner = (z, 2 * yy + 1 - core)
    devs = [place((r + o) % 8, core if k == 0 else 1 - core) for o in range(8) for k in range(2)]

    in_x = pltpu.make_async_copy(x, xg.at[0], isem.at[0])
    in_dy = pltpu.make_async_copy(dy, dyg.at[0], isem.at[1])
    in_x.start()
    in_dy.start()
    barrier = pltpu.get_barrier_semaphore()
    for o, k in PEERS:
        dev = devs[2 * o + k]
        pl.semaphore_signal(barrier, inc=1, device_id={'row': dev[0], 'col': dev[1]},
                            device_id_type=pl.DeviceIdType.MESH)
    both = jnp.concatenate([ridx[...].astype(F32), gates[...]], axis=1)
    meta[...] = both
    mg[0] = both
    in_x.wait()
    in_dy.wait()
    pl.semaphore_wait(barrier, ND - 1)

    gath = (xg, dyg)

    def own(t, d, m):
        h = m if d == 0 else NC - 1 - m
        rows = slice(h * CH, h * CH + CH)
        return remote(gath[t].at[0, rows], gath[t].at[14 if d == 0 else 2, rows], ags.at[t, d, m], agr.at[t, d, m], nbr[d])

    def piece(d, m):
        k = 1 + lax.div(m, NC)
        h = lax.rem(m, NC) if d == 0 else NC - 1 - lax.rem(m, NC)
        return (8 - k) if d == 0 else k, pl.ds(pl.multiple_of(h * CH, CH), CH)

    def here(t, d, m):
        c = gath[t].at[0, :CH]
        return remote(c, c, ags.at[t, d, m], agr.at[t, d, m], nbr[d])

    def onward(t, d, m):
        o, rows = piece(d, m)
        return remote(gath[t].at[2 * o, rows], gath[t].at[2 * (o - 1 if d == 0 else o + 1), rows],
                      ags.at[t, d, m + NC], agr.at[t, d, m + NC], nbr[d])

    def across(t, d, m):
        o, rows = piece(d, m)
        return remote(gath[t].at[2 * o, rows], gath[t].at[2 * o + 1, rows], pgs.at[t, d, m], pgr.at[t, d, m], partner)

    def crossed(t, d, m):
        c = gath[t].at[0, :CH]
        return remote(c, c, pgs.at[t, d, m], pgr.at[t, d, m], partner)

    def own_across(t):
        return remote(gath[t].at[0], gath[t].at[1], pgs.at[t, 0, LAST], pgr.at[t, 0, LAST], partner)

    def ag_start(t):
        for m in range(NC):
            for d in range(2):
                own(t, d, m).start()
        own_across(t).start()

    def ag_step(t, m):
        for d in range(2):
            here(t, d, m).wait_recv()
            if isinstance(m, int):
                if m < LAST - NC:
                    onward(t, d, m).start()
            else:
                @pl.when(m < LAST - NC)
                def _():
                    onward(t, d, m).start()
            across(t, d, m).start()

    def ag_crossed(t, lo, hi):
        for m in range(lo, hi):
            for d in range(2):
                crossed(t, d, m).wait_recv()

    def meta_copy(o, k):
        return remote(meta, mg.at[2 * ((8 - o) % 8) + k], ms.at[2 * o + k], mr.at[2 * ((8 - o) % 8) + k], devs[2 * o + k])

    def meta_wait(o, k):
        return remote(meta, mg.at[0], ms.at[2 * o + k], mr.at[2 * o + k], devs[2 * o + k])

    for o, k in PEERS:
        meta_copy(o, k).start()
    ag_start(0)

    def gather_block(src, b):
        p = jnp.where(select(code, b), 1.0, 0.0).astype(BF)
        xrow[b] = dot(p, src[pl.ds(NB * b, NB)].reshape(TB, D)).astype(BF)

    def xload(m, _):
        ag_step(0, m)

        @pl.when(m > 0)
        def _():
            load13(m - 1)
        return 0

    def load13(e):
        pltpu.make_async_copy(w1h.at[e], w1.at[e], wsem.at[e, 0]).start()
        pltpu.make_async_copy(w3h.at[e], w3.at[e], wsem.at[e, 1]).start()

    lax.fori_loop(0, 3, xload, 0)
    for o, k in PEERS:
        meta_wait(o, k).wait_recv()

    def xstep(m, _):
        ag_step(0, m)
        load13(m - 1)

        @pl.when(m < 7)
        def _():
            put_codes(m - 3, base, mg, code, gate)

        @pl.when(m > 6)
        def _():
            put_tables(m - 7, code, gate, gs, tab)
        return 0

    lax.fori_loop(3, 9, xstep, 0)
    ag_step(0, 9)
    ag_start(1)
    put_tables(2, code, gate, gs, tab)
    ag_step(0, 10)
    ag_step(0, 11)
    for e in range(EL):
        pltpu.make_async_copy(w2h.at[e], w2.at[e], wsem.at[e, 2]).start()
    put_tables(3, code, gate, gs, tab)
    own_across(0).wait_recv()
    ag_crossed(0, 0, NC)
    gather_block(xg, 0)
    ag_step(0, 12)
    ag_crossed(0, NC, 2 * NC)
    gather_block(xg, 3)
    ag_step(0, 13)
    ag_crossed(0, 2 * NC, 3 * NC)
    gather_block(xg, 1)
    ag_step(1, 0)
    ag_step(1, 1)
    ag_crossed(0, 3 * NC, LAST)
    gather_block(xg, 2)
    ag_step(1, 2)
    ag_step(1, 3)

    def rows_of(ref, e):
        return ref[:, pl.ds(pl.multiple_of(e * RB, RB), RB), :]

    def put_rows(ref, e, v):
        ref[:, pl.ds(pl.multiple_of(e * RB, RB), RB), :] = v.reshape(NB, RB, v.shape[-1])

    out_x = pltpu.make_async_copy(xrow, xrh, osem.at[0])
    out_x.start()

    def fwd(e, _):
        pltpu.make_async_copy(w1h.at[e], w1.at[e], wsem.at[e, 0]).wait()
        pltpu.make_async_copy(w3h.at[e], w3.at[e], wsem.at[e, 1]).wait()
        xe = rows_of(xrow, e).reshape(NB * RB, D)
        u = dot(xe, w1[e]).astype(BF)
        v = dot(xe, w3[e]).astype(BF)
        us[e] = u
        vs[e] = v
        uf = u.astype(F32)
        av[e] = (uf * jax.nn.sigmoid(uf) * v.astype(F32)).astype(BF)
        ag_step(1, e + NC)
        return 0

    lax.fori_loop(0, EL, fwd, 0)
    out_a = pltpu.make_async_copy(av, arh, osem.at[1])
    out_a.start()

    def rs_pair(t, o):
        return remote(acc.at[t, 2 * o + 1], pbuf.at[t, o], rps.at[t, o], rpr.at[t, o], partner)

    def rs_join(t, o):
        rs_pair(t, o).wait_recv()
        acc[t, 2 * o] = acc[t, 2 * o] + pbuf[t, o]

    def rs_got(t, d, m):
        return remote(acc.at[0, 0, :HALF], rbuf.at[0, 0, 0], rss.at[t, d, m], rsr.at[t, d, m], nbr[d])

    def rs_move(t, d, m):
        dist = 4 - lax.div(m + 1, 2)
        h = lax.rem(m, 2) if d == 0 else 1 - lax.rem(m, 2)
        o = dist if d == 0 else 8 - dist
        rows = pl.ds(pl.multiple_of(h * HALF, HALF), HALF)
        return 2 * o, rows, remote(acc.at[t, 2 * o, rows], rbuf.at[t, d, m], rss.at[t, d, m], rsr.at[t, d, m], nbr[d])

    def rs_first(t):
        rs_join(t, 4)
        for d in range(2):
            rs_move(t, d, 0)[2].start()
        rs_join(t, 3)
        rs_join(t, 5)
        for d in range(2):
            rs_move(t, d, 1)[2].start()
        for o in (2, 6, 1, 7, 0):
            rs_join(t, o)

    def rs_step(t, m):
        for d in range(2):
            rs_got(t, d, m - 2).wait_recv()
            p, rows, copy = rs_move(t, d, m)
            acc[t, p, rows] = acc[t, p, rows] + rbuf[t, d, m - 2]
            copy.start()

    def rs_last(t, out):
        cols = slice((t % 2) * DH, (t % 2) * DH + DH)
        for m in (5, 6):
            for d in range(2):
                rs_got(t, d, m).wait_recv()
        out[:HALF, cols] = (acc[t, 0, :HALF] + rbuf[t, 0, 6] + rbuf[t, 1, 5]).astype(BF)
        out[HALF:, cols] = (acc[t, 0, HALF:] + rbuf[t, 0, 5] + rbuf[t, 1, 6]).astype(BF)

    def forward_half(c):
        cols = slice(c * DH, c * DH + DH)

        def out(e, _):
            if c == 0:
                pltpu.make_async_copy(w2h.at[e], w2.at[e], wsem.at[e, 2]).wait()
            orow[:, pl.ds(pl.multiple_of(e * RB, RB), RB), cols] = dot(av[e], w2[e, :, cols]).astype(BF).reshape(NB, RB, DH)
            return 0

        lax.fori_loop(0, EL, out, 0)
        if c == 0:
            ag_step(1, 12)
            ag_step(1, 13)

        def scatter(i, _):
            b = lax.rem(i + 2, NB)
            o = orow[b, :, cols]
            acc[c, pl.ds(NB * b, NB)] = (dot(tab[b, 0], o) + dot(tab[b, 1], o) + dot(tab[b, 2], o)).reshape(NB, TOK, DH)
            rs_pair(c, 2 * b).start()
            rs_pair(c, 2 * b + 1).start()
            if c == 1:
                for at, m in ((1, 2), (3, 3)):
                    @pl.when(i == at)
                    def _():
                        rs_step(0, m)
            return 0

        lax.fori_loop(0, NB, scatter, 0)
        rs_first(c)

    forward_half(0)
    forward_half(1)
    own_across(1).wait_recv()
    ag_crossed(1, 0, LAST)
    out_x.wait()

    def gather_dy(b, _):
        gather_block(dyg, b)
        return 0

    lax.fori_loop(0, NB, gather_dy, 0)
    rs_step(0, 4)

    def bwd(e, _):
        dye = rows_of(xrow, e).reshape(NB * RB, D).astype(F32)
        o = rows_of(orow, e).reshape(NB * RB, D).astype(F32)
        put_rows(ds, e, jnp.sum(dye * o, axis=1, keepdims=True))
        g = rows_of(gs, e).reshape(NB * RB, 1)
        do = (g * dye).astype(BF)
        put_rows(xrow, e, do)
        da = dot_nt(do, w2[e])
        u = us[e].astype(F32)
        v = vs[e].astype(F32)
        s = jax.nn.sigmoid(u)
        du = (da * v * s * (1.0 + u * (1.0 - s))).astype(BF)
        dv = (da * u * s).astype(BF)
        us[e] = du
        vs[e] = dv
        for at, t, m in ((1, 0, 5), (3, 1, 2), (5, 1, 3), (7, 0, 6)):
            @pl.when(e == at)
            def _():
                rs_step(t, m)
        return 0

    lax.fori_loop(0, EL, bwd, 0)
    outs = [pltpu.make_async_copy(xrow, dorh, osem.at[2]), pltpu.make_async_copy(us, durh, osem.at[3]),
            pltpu.make_async_copy(vs, dvrh, osem.at[4])]
    for c in outs:
        c.start()

    def slots_back(b, _):
        dg = jnp.where(select(code, b), ds[b], 0.0)
        dge = jnp.concatenate([jnp.sum(dg[e * RB:(e + 1) * RB], axis=0, keepdims=True) for e in range(EL)], axis=0)
        for i in range(NB):
            dgs[NB * b + i, :, :TOK] = dge[:, i * TOK:(i + 1) * TOK]
        return 0

    lax.fori_loop(0, NB, slots_back, 0)

    def dg_copy(o, k):
        return remote(dgs.at[2 * o + k], dgr.at[2 * ((8 - o) % 8) + k], gss.at[2 * o + k], gsr.at[2 * ((8 - o) % 8) + k],
                      devs[2 * o + k])

    def dg_wait(o, k):
        return remote(dgs.at[0], dgr.at[0], gss.at[2 * o + k], gsr.at[2 * o + k], devs[2 * o + k])

    for o, k in PEERS:
        dg_copy(o, k).start()
    dgr[0] = dgs[0]

    def backward_half(c):
        cols = slice(c * DH, c * DH + DH)

        def back(e, _):
            dx = dot_nt(us[e], w1[e, cols, :]) + dot_nt(vs[e], w3[e, cols, :])
            orow[:, pl.ds(pl.multiple_of(e * RB, RB), RB), cols] = dx.astype(BF).reshape(NB, RB, DH)
            if c == 0:
                for at, m in ((3, 4), (7, 5)):
                    @pl.when(e == at)
                    def _():
                        rs_step(1, m)
            return 0

        lax.fori_loop(0, EL, back, 0)

        def scatter(i, _):
            b = lax.rem(i + 2, NB)
            acc[2 + c, pl.ds(NB * b, NB)] = dot(tab[b, 3], orow[b, :, cols]).reshape(NB, TOK, DH)
            rs_pair(2 + c, 2 * b).start()
            rs_pair(2 + c, 2 * b + 1).start()
            return 0

        lax.fori_loop(0, NB, scatter, 0)
        rs_first(2 + c)

    backward_half(0)
    rs_step(1, 6)
    backward_half(1)

    rs_step(2, 2)
    rs_step(2, 3)
    rs_step(3, 2)
    rs_last(0, yo)
    rs_step(3, 3)
    rs_last(1, yo)
    rs_step(2, 4)
    rs_step(2, 5)
    rs_step(3, 4)
    rs_step(3, 5)
    for o, k in PEERS:
        dg_wait(o, k).wait_recv()
    lane = lax.broadcasted_iota(jnp.int32, (EL, TOK), 0)
    total = [jnp.zeros((EL, TOK), F32)] * TOP
    for i in range(ND):
        expert = lane + (devs[i][0] * 4 + devs[i][1]) * EL
        back = dgr[i, :, :TOK]
        total = [t + jnp.where(expert == ridx[j:j + 1], back, 0.0) for j, t in enumerate(total)]
    dgo[...] = jnp.concatenate([jnp.sum(t, axis=0, keepdims=True) for t in total], axis=0)
    for t in range(2):
        own_across(t).wait_send()
        for m in range(LAST):
            for d in range(2):
                here(t, d, m).wait_send()
                crossed(t, d, m).wait_send()
    for o, k in PEERS:
        meta_wait(o, k).wait_send()
        dg_wait(o, k).wait_send()
    out_a.wait()
    rs_step(2, 6)
    for c in outs:
        c.wait()
    for t in range(4):
        for o in range(8):
            rs_pair(t, o).wait_send()
    rs_step(3, 6)
    for t in range(2):
        for m in range(7):
            for d in range(2):
                rs_got(t, d, m).wait_send()
    rs_last(2, dxo)
    rs_last(3, dxo)
    for t in range(2, 4):
        for m in range(7):
            for d in range(2):
                rs_got(t, d, m).wait_send()


def main(ridx, gates, x, dy, w1, w3, w2):
    vm = pl.BlockSpec(memory_space=pltpu.VMEM)
    hb = pl.BlockSpec(memory_space=pl.ANY)
    sds = jax.ShapeDtypeStruct
    R = NB * RB
    dma = lambda *s: pltpu.SemaphoreType.DMA(s)
    return pl.pallas_call(
        main_kernel,
        out_shape=(sds((TOK, D), BF), sds((TOK, D), BF), sds((TOP, TOK), F32),
                   sds((NB, EL * RB, D), BF), sds((NB, EL * RB, D), BF), sds((EL, R, FF), BF), sds((EL, R, FF), BF), sds((EL, R, FF), BF)),
        in_specs=[vm, vm, hb, hb, hb, hb, hb],
        out_specs=[vm, vm, vm] + [hb] * 5,
        scratch_shapes=[
            pltpu.VMEM((EL, D, FF), BF), pltpu.VMEM((EL, D, FF), BF), pltpu.VMEM((EL, FF, D), BF),
            dma(EL, 3), dma(5), dma(2), pltpu.VMEM((TOP, 128), F32),
            pltpu.VMEM((ND, TOK, D), BF), pltpu.VMEM((ND, TOK, D), BF), pltpu.VMEM((ND, TOP, 128), F32),
            pltpu.VMEM((NB, EL, TB), jnp.int32), pltpu.VMEM((NB, EL, TB), F32), pltpu.VMEM((NB, 4, TB, EL * RB), BF),
            pltpu.VMEM((NB, EL * RB, D), BF), pltpu.VMEM((NB, EL * RB, D), BF),
            pltpu.VMEM((EL, R, FF), BF), pltpu.VMEM((EL, R, FF), BF), pltpu.VMEM((EL, R, FF), BF),
            pltpu.VMEM((NB, EL * RB, 1), F32), pltpu.VMEM((NB, EL * RB, 1), F32),
            pltpu.VMEM((4, ND, TOK, DH), F32), pltpu.VMEM((4, 8, TOK, DH), F32), pltpu.VMEM((4, 2, 7, HALF, DH), F32),
            pltpu.VMEM((ND, EL, 128), F32), pltpu.VMEM((ND, EL, 128), F32),
            dma(2, 2, LAST), dma(2, 2, LAST), dma(2, 2, LAST + 1), dma(2, 2, LAST + 1), dma(ND), dma(ND), dma(ND), dma(ND),
            dma(4, 2, 7), dma(4, 2, 7), dma(4, 8), dma(4, 8),
        ],
        compiler_params=pltpu.CompilerParams(vmem_limit_bytes=VMEM_LIMIT, collective_id=0, has_side_effects=True),
        name='moe',
    )(ridx, gates, x, dy, w1, w3, w2)


def dw_kernel(y, dx, dg, x, do, a, du, dv, yo, dxo, dgo, g1, g3, g2):
    @pl.when(pl.program_id(0) == 0)
    def _():
        yo[...] = y[...]
        dxo[...] = dx[...]
        dgo[...] = dg[...]
    xb = x[...].reshape(NB * RB, D)
    g1[0] = dot_tn(xb, du[0])
    g3[0] = dot_tn(xb, dv[0])
    g2[0] = dot_tn(a[0], do[...].reshape(NB * RB, D))


def dw(y, dx, dg, xr, dor, ar, dur, dvr):
    sds = jax.ShapeDtypeStruct
    R = NB * RB
    whole = lambda *s: pl.BlockSpec(s, lambda e: (0, 0))
    act = pl.BlockSpec((1, R, FF), lambda e: (e, 0, 0))
    br = pl.BlockSpec((NB, RB, D), lambda e: (0, e, 0))
    same = [whole(TOK, D), whole(TOK, D), whole(TOP, TOK)]
    return pl.pallas_call(
        dw_kernel,
        grid=(EL,),
        out_shape=(sds((TOK, D), BF), sds((TOK, D), BF), sds((TOP, TOK), F32),
                   sds((EL, D, FF), F32), sds((EL, D, FF), F32), sds((EL, FF, D), F32)),
        in_specs=same + [br, br, act, act, act],
        out_specs=same + [pl.BlockSpec((1, D, FF), lambda e: (e, 0, 0)), pl.BlockSpec((1, D, FF), lambda e: (e, 0, 0)),
                          pl.BlockSpec((1, FF, D), lambda e: (e, 0, 0))],
        name='dw',
    )(y, dx, dg, xr, dor, ar, dur, dvr)


def solution(mesh):
    grp = ('row', 'col')
    tspec = P(('dp', 'row', 'col'), None)
    wspec = P(grp, None, None)
    gspec = P(('dp', 'row', 'col'), None, None)

    def local(x, ridx, gates, w1, w3, w2, dy):
        y, dx, dg, g1, g3, g2 = dw(*main(ridx.T, gates.T, x, dy, w1, w3, w2))
        return y, dx, dg.T, g1, g3, g2

    return jax.shard_map(local, mesh=mesh, in_specs=(tspec, tspec, tspec, wspec, wspec, wspec, tspec),
                         out_specs=(tspec, tspec, tspec, gspec, gspec, gspec), check_vma=False)
```

time: 110 us -> 105 us (0.955)
  Pallas kernels: 108 us -> 104 us
    pallas_call x1, Pallas kernels: 90.6 us -> 86.3 us  [main(): pl.pallas_call(main_kernel, out_shape=(sds((TOK, D), BF), sds((TOK, D), B...]
where the time goes in v5:
time: 105 us
  Pallas kernels  104 us (99%)
    pallas_call x1, Pallas kernels, main(): pl.pallas_call(main_kernel, out_shape=(sds((TOK, D), BF), sds((TOK, D), B...  86.3 us
    pallas_call x1, Pallas kernels, dw(): pl.pallas_call(dw_kernel, grid=(EL,), out_shape=(sds((TOK, D), BF), sds((...  17.9 us

profile of v5, /device:TPU:0, one launch (start us, length us, event | category | flops | bytes accessed | tf_op | source)
XLA Modules:
  0.0 104.8 jit_solution(3839104643895100780)
XLA Ops:
  0.6 86.3 %moe.1 = (bf16[64,1024]{1,0:T(8,128)(2,1)}, bf16[64,1024]{1,0:T(8,128)(2,1)}, f32[8,64]{1,0:T(8,128)}, bf16[4,512,1024]{2,1,0:T(8,128)(2,1)}, bf16[4,512,1024]{2...) custom-call(s32[8,64]{1,0:T(8,128)} %bitcast.3, ...), custom_call_target="tpu_custom_call" | custom-call | tf_op jit(solution)/shard_map/moe/pallas_call | solution.py:496
  86.9 17.9 %dw.1 = (bf16[64,1024]{1,0:T(8,128)(2,1)}, bf16[64,1024]{1,0:T(8,128)(2,1)}, f32[8,64]{1,0:T(8,128)}, f32[8,1024,384]{2,1,0:T(8,128)}, f32[8,1024,384]{2,1,0:T(8,128)}, /*index=5*/f32[8,384,1024]{2,1,0:T(8,128)}) custom-call(bf16[64,1024]{1,0:T(8,128)(2,1)} %get-tuple-element.20.y, bf16[64,1024]{1,0:T(8,128)(2,1)} %get-tuple-element.21.dx, ...), custom_call_target="tpu_custom_call" | custom-call | tf_op jit(solution)/shard_map/dw/pallas_call | solution.py:539

commit v6 on v5

--- a/solution.py
+++ b/solution.py
@@ -98,8 +98,8 @@
 PEERS = [(o, k) for o in range(8) for k in range(2)][1:]
 
 
-def main_kernel(ridx, gates, x, dy, w1h, w3h, w2h, yo, dxo, dgo, xrh, dorh, arh, durh, dvrh,
-                w1, w3, w2, wsem, osem, isem, meta, xg, dyg, mg, code, gate, tab, xrow, orow, us, vs, av, gs, ds,
+def main_kernel(ridxh, gatesh, x, dy, w1h, w3h, w2h, yo, dxo, dgo, xrh, dorh, arh, durh, dvrh,
+                w1, w3, w2, wsem, osem, isem, ridx, gates, meta, xg, dyg, mg, code, gate, tab, xrow, orow, us, vs, av, gs, ds,
                 acc, pbuf, rbuf, dgs, dgr,
                 ags, agr, pgs, pgr, ms, mr, gss, gsr, rss, rsr, rps, rpr):
     z = lax.axis_index('row')
@@ -114,6 +114,10 @@
 
     in_x = pltpu.make_async_copy(x, xg.at[0], isem.at[0])
     in_dy = pltpu.make_async_copy(dy, dyg.at[0], isem.at[1])
+    in_r = pltpu.make_async_copy(ridxh, ridx, isem.at[2])
+    in_g = pltpu.make_async_copy(gatesh, gates, isem.at[3])
+    in_r.start()
+    in_g.start()
     in_x.start()
     in_dy.start()
     barrier = pltpu.get_barrier_semaphore()
@@ -121,6 +125,8 @@
         dev = devs[2 * o + k]
         pl.semaphore_signal(barrier, inc=1, device_id={'row': dev[0], 'col': dev[1]},
                             device_id_type=pl.DeviceIdType.MESH)
+    in_r.wait()
+    in_g.wait()
     both = jnp.concatenate([ridx[...].astype(F32), gates[...]], axis=1)
     meta[...] = both
     mg[0] = both
@@ -209,7 +215,7 @@
         pltpu.make_async_copy(w1h.at[e], w1.at[e], wsem.at[e, 0]).start()
         pltpu.make_async_copy(w3h.at[e], w3.at[e], wsem.at[e, 1]).start()
 
-    lax.fori_loop(0, 3, xload, 0)
+    lax.fori_loop(0, 5, xload, 0)
     for o, k in PEERS:
         meta_wait(o, k).wait_recv()
 
@@ -217,23 +223,19 @@
         ag_step(0, m)
         load13(m - 1)
 
-        @pl.when(m < 7)
-        def _():
-            put_codes(m - 3, base, mg, code, gate)
-
-        @pl.when(m > 6)
-        def _():
-            put_tables(m - 7, code, gate, gs, tab)
+        put_codes(m - 5, base, mg, code, gate)
         return 0
 
-    lax.fori_loop(3, 9, xstep, 0)
+    lax.fori_loop(5, 9, xstep, 0)
     ag_step(0, 9)
     ag_start(1)
-    put_tables(2, code, gate, gs, tab)
+    put_tables(0, code, gate, gs, tab)
     ag_step(0, 10)
-    ag_step(0, 11)
     for e in range(EL):
         pltpu.make_async_copy(w2h.at[e], w2.at[e], wsem.at[e, 2]).start()
+    put_tables(1, code, gate, gs, tab)
+    ag_step(0, 11)
+    put_tables(2, code, gate, gs, tab)
     put_tables(3, code, gate, gs, tab)
     own_across(0).wait_recv()
     ag_crossed(0, 0, NC)
@@ -410,6 +412,7 @@
         dg_copy(o, k).start()
     dgr[0] = dgs[0]
 
+
     def backward_half(c):
         cols = slice(c * DH, c * DH + DH)
 
@@ -421,6 +424,10 @@
                     @pl.when(e == at)
                     def _():
                         rs_step(1, m)
+            else:
+                @pl.when(e == 7)
+                def _():
+                    rs_step(2, 2)
             return 0
 
         lax.fori_loop(0, EL, back, 0)
@@ -430,6 +437,10 @@
             acc[2 + c, pl.ds(NB * b, NB)] = dot(tab[b, 3], orow[b, :, cols]).reshape(NB, TOK, DH)
             rs_pair(2 + c, 2 * b).start()
             rs_pair(2 + c, 2 * b + 1).start()
+            if c == 1:
+                @pl.when(i == 2)
+                def _():
+                    rs_step(2, 3)
             return 0
 
         lax.fori_loop(0, NB, scatter, 0)
@@ -439,25 +450,15 @@
     rs_step(1, 6)
     backward_half(1)
 
-    rs_step(2, 2)
-    rs_step(2, 3)
+    rs_last(0, yo)
+    rs_step(2, 4)
+    rs_last(1, yo)
+    rs_step(2, 5)
     rs_step(3, 2)
-    rs_last(0, yo)
     rs_step(3, 3)
-    rs_last(1, yo)
-    rs_step(2, 4)
-    rs_step(2, 5)
+    rs_step(2, 6)
     rs_step(3, 4)
     rs_step(3, 5)
-    for o, k in PEERS:
-        dg_wait(o, k).wait_recv()
-    lane = lax.broadcasted_iota(jnp.int32, (EL, TOK), 0)
-    total = [jnp.zeros((EL, TOK), F32)] * TOP
-    for i in range(ND):
-        expert = lane + (devs[i][0] * 4 + devs[i][1]) * EL
-        back = dgr[i, :, :TOK]
-        total = [t + jnp.where(expert == ridx[j:j + 1], back, 0.0) for j, t in enumerate(total)]
-    dgo[...] = jnp.concatenate([jnp.sum(t, axis=0, keepdims=True) for t in total], axis=0)
     for t in range(2):
         own_across(t).wait_send()
         for m in range(LAST):
@@ -466,9 +467,7 @@
                 crossed(t, d, m).wait_send()
     for o, k in PEERS:
         meta_wait(o, k).wait_send()
-        dg_wait(o, k).wait_send()
     out_a.wait()
-    rs_step(2, 6)
     for c in outs:
         c.wait()
     for t in range(4):
@@ -481,6 +480,17 @@
                 rs_got(t, d, m).wait_send()
     rs_last(2, dxo)
     rs_last(3, dxo)
+    for o, k in PEERS:
+        dg_wait(o, k).wait_recv()
+    lane = lax.broadcasted_iota(jnp.int32, (EL, TOK), 0)
+    total = [jnp.zeros((EL, TOK), F32)] * TOP
+    for i in range(ND):
+        expert = lane + (devs[i][0] * 4 + devs[i][1]) * EL
+        back = dgr[i, :, :TOK]
+        total = [t + jnp.where(expert == ridx[j:j + 1], back, 0.0) for j, t in enumerate(total)]
+    dgo[...] = jnp.concatenate([jnp.sum(t, axis=0, keepdims=True) for t in total], axis=0)
+    for o, k in PEERS:
+        dg_wait(o, k).wait_send()
     for t in range(2, 4):
         for m in range(7):
             for d in range(2):
@@ -497,11 +507,11 @@
         main_kernel,
         out_shape=(sds((TOK, D), BF), sds((TOK, D), BF), sds((TOP, TOK), F32),
                    sds((NB, EL * RB, D), BF), sds((NB, EL * RB, D), BF), sds((EL, R, FF), BF), sds((EL, R, FF), BF), sds((EL, R, FF), BF)),
-        in_specs=[vm, vm, hb, hb, hb, hb, hb],
+        in_specs=[hb] * 7,
         out_specs=[vm, vm, vm] + [hb] * 5,
         scratch_shapes=[
             pltpu.VMEM((EL, D, FF), BF), pltpu.VMEM((EL, D, FF), BF), pltpu.VMEM((EL, FF, D), BF),
-            dma(EL, 3), dma(5), dma(2), pltpu.VMEM((TOP, 128), F32),
+            dma(EL, 3), dma(5), dma(4), pltpu.VMEM((TOP, TOK), jnp.int32), pltpu.VMEM((TOP, TOK), F32), pltpu.VMEM((TOP, 128), F32),
             pltpu.VMEM((ND, TOK, D), BF), pltpu.VMEM((ND, TOK, D), BF), pltpu.VMEM((ND, TOP, 128), F32),
             pltpu.VMEM((NB, EL, TB), jnp.int32), pltpu.VMEM((NB, EL, TB), F32), pltpu.VMEM((NB, 4, TB, EL * RB), BF),
             pltpu.VMEM((NB, EL * RB, D), BF), pltpu.VMEM((NB, EL * RB, D), BF),
@@ -517,16 +527,30 @@
     )(ridx, gates, x, dy, w1, w3, w2)
 
 
-def dw_kernel(y, dx, dg, x, do, a, du, dv, yo, dxo, dgo, g1, g3, g2):
-    @pl.when(pl.program_id(0) == 0)
+def dw_kernel(y, dx, dg, x, do, a, du, dv, yo, dxo, dgo, g1, g3, g2, b1, b3, b2, sem):
+    e = pl.program_id(0)
+    slot = lax.rem(e, 2)
+    xb = x[...].reshape(NB * RB, D)
+    made = ((g1, b1, lambda: dot_tn(xb, du[0])), (g3, b3, lambda: dot_tn(xb, dv[0])),
+            (g2, b2, lambda: dot_tn(a[0], do[...].reshape(NB * RB, D))))
+    for i, (out, buf, make) in enumerate(made):
+        @pl.when(e >= 2)
+        def _():
+            pltpu.make_async_copy(buf.at[slot], out.at[e - 2], sem.at[i, slot]).wait()
+        buf[slot] = make()
+        pltpu.make_async_copy(buf.at[slot], out.at[e], sem.at[i, slot]).start()
+
+    @pl.when(e == 0)
     def _():
         yo[...] = y[...]
         dxo[...] = dx[...]
         dgo[...] = dg[...]
-    xb = x[...].reshape(NB * RB, D)
-    g1[0] = dot_tn(xb, du[0])
-    g3[0] = dot_tn(xb, dv[0])
-    g2[0] = dot_tn(a[0], do[...].reshape(NB * RB, D))
+
+    @pl.when(e == EL - 1)
+    def _():
+        for i, (out, buf, make) in enumerate(made):
+            pltpu.make_async_copy(buf.at[1 - slot], out.at[e - 1], sem.at[i, 1 - slot]).wait()
+            pltpu.make_async_copy(buf.at[slot], out.at[e], sem.at[i, slot]).wait()
 
 
 def dw(y, dx, dg, xr, dor, ar, dur, dvr):
@@ -542,8 +566,9 @@
         out_shape=(sds((TOK, D), BF), sds((TOK, D), BF), sds((TOP, TOK), F32),
                    sds((EL, D, FF), F32), sds((EL, D, FF), F32), sds((EL, FF, D), F32)),
         in_specs=same + [br, br, act, act, act],
-        out_specs=same + [pl.BlockSpec((1, D, FF), lambda e: (e, 0, 0)), pl.BlockSpec((1, D, FF), lambda e: (e, 0, 0)),
-                          pl.BlockSpec((1, FF, D), lambda e: (e, 0, 0))],
+        out_specs=same + [pl.BlockSpec(memory_space=pl.ANY)] * 3,
+        scratch_shapes=[pltpu.VMEM((2, D, FF), F32), pltpu.VMEM((2, D, FF), F32), pltpu.VMEM((2, FF, D), F32),
+                        pltpu.SemaphoreType.DMA((3, 2))],
         name='dw',
     )(y, dx, dg, xr, dor, ar, dur, dvr)
 

time: 105 us -> 105 us (level)
  no operation moved by 1% of the time
where the time goes in v6:
time: 105 us; the launch traced here: 104 us
  Pallas kernels  104 us (99%)
    pallas_call x1, Pallas kernels, main(): pl.pallas_call(main_kernel, out_shape=(sds((TOK, D), BF), sds((TOK, D), B...  85.4 us
    pallas_call x1, Pallas kernels, dw(): pl.pallas_call(dw_kernel, grid=(EL,), out_shape=(sds((TOK, D), BF), sds((...  18.3 us

profile of v6, /device:TPU:0, one launch (start us, length us, event | category | flops | bytes accessed | tf_op | source)
XLA Modules:
  0.0 104.4 jit_solution(13204984725622293096)
XLA Ops:
  0.6 85.4 %moe.1 = (bf16[64,1024]{1,0:T(8,128)(2,1)}, bf16[64,1024]{1,0:T(8,128)(2,1)}, f32[8,64]{1,0:T(8,128)}, bf16[4,512,1024]{2,1,0:T(8,128)(2,1)}, bf16[4,512,1024]{2...) custom-call(s32[8,64]{1,0:T(8,128)} %bitcast.3, ...), custom_call_target="tpu_custom_call" | custom-call | tf_op jit(solution)/shard_map/moe/pallas_call | solution.py:506
  86.1 18.3 %dw.1 = (bf16[64,1024]{1,0:T(8,128)(2,1)}, bf16[64,1024]{1,0:T(8,128)(2,1)}, f32[8,64]{1,0:T(8,128)}, f32[8,1024,384]{2,1,0:T(8,128)}, f32[8,1024,384]{2,1,0:T(8,128)}, /*index=5*/f32[8,384,1024]{2,1,0:T(8,128)}) custom-call(bf16[64,1024]{1,0:T(8,128)(2,1)} %get-tuple-element.20.y, bf16[64,1024]{1,0:T(8,128)(2,1)} %get-tuple-element.21.dx, ...), custom_call_target="tpu_custom_call" | custom-call | tf_op jit(solution)/shard_map/dw/pallas_call | solution.py:563

commit v7 on v6

--- a/solution.py
+++ b/solution.py
@@ -90,7 +90,8 @@
         device_id={'row': dev[0], 'col': dev[1]}, device_id_type=pl.DeviceIdType.MESH)
 
 
-HALF = TOK // 2
+QR = TOK // 4
+NR = 14
 NC = 4
 CH = TOK // NC
 LAST = 3 * NC + NC // 2
@@ -286,41 +287,47 @@
         rs_pair(t, o).wait_recv()
         acc[t, 2 * o] = acc[t, 2 * o] + pbuf[t, o]
 
-    def rs_got(t, d, m):
-        return remote(acc.at[0, 0, :HALF], rbuf.at[0, 0, 0], rss.at[t, d, m], rsr.at[t, d, m], nbr[d])
-
-    def rs_move(t, d, m):
-        dist = 4 - lax.div(m + 1, 2)
-        h = lax.rem(m, 2) if d == 0 else 1 - lax.rem(m, 2)
+    def rs_got(t, d, q):
+        return remote(acc.at[0, 0, :QR], rbuf.at[0, 0, 0], rss.at[t, d, q], rsr.at[t, d, q], nbr[d])
+
+    def rs_move(t, d, q):
+        dist = 4 - (q + 2) // 4
+        h = q % 4 if d == 0 else 3 - q % 4
         o = dist if d == 0 else 8 - dist
-        rows = pl.ds(pl.multiple_of(h * HALF, HALF), HALF)
-        return 2 * o, rows, remote(acc.at[t, 2 * o, rows], rbuf.at[t, d, m], rss.at[t, d, m], rsr.at[t, d, m], nbr[d])
+        rows = slice(h * QR, h * QR + QR)
+        return 2 * o, rows, remote(acc.at[t, 2 * o, rows], rbuf.at[t, d, q], rss.at[t, d, q], rsr.at[t, d, q], nbr[d])
 
     def rs_first(t):
         rs_join(t, 4)
-        for d in range(2):
-            rs_move(t, d, 0)[2].start()
+        for q in range(2):
+            for d in range(2):
+                rs_move(t, d, q)[2].start()
         rs_join(t, 3)
         rs_join(t, 5)
-        for d in range(2):
-            rs_move(t, d, 1)[2].start()
+        for q in range(2, 4):
+            for d in range(2):
+                rs_move(t, d, q)[2].start()
+
+    def rs_rest(t):
         for o in (2, 6, 1, 7, 0):
             rs_join(t, o)
 
     def rs_step(t, m):
-        for d in range(2):
-            rs_got(t, d, m - 2).wait_recv()
-            p, rows, copy = rs_move(t, d, m)
-            acc[t, p, rows] = acc[t, p, rows] + rbuf[t, d, m - 2]
-            copy.start()
+        for q in (2 * m, 2 * m + 1):
+            for d in range(2):
+                rs_got(t, d, q - 4).wait_recv()
+                p, rows, copy = rs_move(t, d, q)
+                acc[t, p, rows] = acc[t, p, rows] + rbuf[t, d, q - 4]
+                copy.start()
 
     def rs_last(t, out):
         cols = slice((t % 2) * DH, (t % 2) * DH + DH)
-        for m in (5, 6):
-            for d in range(2):
-                rs_got(t, d, m).wait_recv()
-        out[:HALF, cols] = (acc[t, 0, :HALF] + rbuf[t, 0, 6] + rbuf[t, 1, 5]).astype(BF)
-        out[HALF:, cols] = (acc[t, 0, HALF:] + rbuf[t, 0, 5] + rbuf[t, 1, 6]).astype(BF)
+        for q in range(NR - 4, NR):
+            for d in range(2):
+                rs_got(t, d, q).wait_recv()
+        for j, (qr, ql) in enumerate(((12, 11), (13, 10), (10, 13), (11, 12))):
+            rows = slice(j * QR, j * QR + QR)
+            out[rows, cols] = (acc[t, 0, rows] + rbuf[t, 0, qr] + rbuf[t, 1, ql]).astype(BF)
 
     def forward_half(c):
         cols = slice(c * DH, c * DH + DH)
@@ -329,6 +336,10 @@
             if c == 0:
                 pltpu.make_async_copy(w2h.at[e], w2.at[e], wsem.at[e, 2]).wait()
             orow[:, pl.ds(pl.multiple_of(e * RB, RB), RB), cols] = dot(av[e], w2[e, :, cols]).astype(BF).reshape(NB, RB, DH)
+            if c == 1:
+                @pl.when(e == 4)
+                def _():
+                    rs_rest(0)
             return 0
 
         lax.fori_loop(0, EL, out, 0)
@@ -337,7 +348,7 @@
             ag_step(1, 13)
 
         def scatter(i, _):
-            b = lax.rem(i + 2, NB)
+            b = lax.rem(3 * i + 2, NB)
             o = orow[b, :, cols]
             acc[c, pl.ds(NB * b, NB)] = (dot(tab[b, 0], o) + dot(tab[b, 1], o) + dot(tab[b, 2], o)).reshape(NB, TOK, DH)
             rs_pair(c, 2 * b).start()
@@ -360,6 +371,10 @@
 
     def gather_dy(b, _):
         gather_block(dyg, b)
+
+        @pl.when(b == 2)
+        def _():
+            rs_rest(1)
         return 0
 
     lax.fori_loop(0, NB, gather_dy, 0)
@@ -392,27 +407,6 @@
     for c in outs:
         c.start()
 
-    def slots_back(b, _):
-        dg = jnp.where(select(code, b), ds[b], 0.0)
-        dge = jnp.concatenate([jnp.sum(dg[e * RB:(e + 1) * RB], axis=0, keepdims=True) for e in range(EL)], axis=0)
-        for i in range(NB):
-            dgs[NB * b + i, :, :TOK] = dge[:, i * TOK:(i + 1) * TOK]
-        return 0
-
-    lax.fori_loop(0, NB, slots_back, 0)
-
-    def dg_copy(o, k):
-        return remote(dgs.at[2 * o + k], dgr.at[2 * ((8 - o) % 8) + k], gss.at[2 * o + k], gsr.at[2 * ((8 - o) % 8) + k],
-                      devs[2 * o + k])
-
-    def dg_wait(o, k):
-        return remote(dgs.at[0], dgr.at[0], gss.at[2 * o + k], gsr.at[2 * o + k], devs[2 * o + k])
-
-    for o, k in PEERS:
-        dg_copy(o, k).start()
-    dgr[0] = dgs[0]
-
-
     def backward_half(c):
         cols = slice(c * DH, c * DH + DH)
 
@@ -425,6 +419,10 @@
                     def _():
                         rs_step(1, m)
             else:
+                @pl.when(e == 3)
+                def _():
+                    rs_rest(2)
+
                 @pl.when(e == 7)
                 def _():
                     rs_step(2, 2)
@@ -433,7 +431,7 @@
         lax.fori_loop(0, EL, back, 0)
 
         def scatter(i, _):
-            b = lax.rem(i + 2, NB)
+            b = lax.rem(3 * i + 2, NB)
             acc[2 + c, pl.ds(NB * b, NB)] = dot(tab[b, 3], orow[b, :, cols]).reshape(NB, TOK, DH)
             rs_pair(2 + c, 2 * b).start()
             rs_pair(2 + c, 2 * b + 1).start()
@@ -449,6 +447,27 @@
     backward_half(0)
     rs_step(1, 6)
     backward_half(1)
+
+    def slots_back(b, _):
+        dg = jnp.where(select(code, b), ds[b], 0.0)
+        dge = jnp.concatenate([jnp.sum(dg[e * RB:(e + 1) * RB], axis=0, keepdims=True) for e in range(EL)], axis=0)
+        for i in range(NB):
+            dgs[NB * b + i, :, :TOK] = dge[:, i * TOK:(i + 1) * TOK]
+        return 0
+
+    lax.fori_loop(0, NB, slots_back, 0)
+
+    def dg_copy(o, k):
+        return remote(dgs.at[2 * o + k], dgr.at[2 * ((8 - o) % 8) + k], gss.at[2 * o + k], gsr.at[2 * ((8 - o) % 8) + k],
+                      devs[2 * o + k])
+
+    def dg_wait(o, k):
+        return remote(dgs.at[0], dgr.at[0], gss.at[2 * o + k], gsr.at[2 * o + k], devs[2 * o + k])
+
+    for o, k in PEERS:
+        dg_copy(o, k).start()
+    dgr[0] = dgs[0]
+    rs_rest(3)
 
     rs_last(0, yo)
     rs_step(2, 4)
@@ -475,9 +494,9 @@
             rs_pair(t, o).wait_send()
     rs_step(3, 6)
     for t in range(2):
-        for m in range(7):
-            for d in range(2):
-                rs_got(t, d, m).wait_send()
+        for q in range(NR):
+            for d in range(2):
+                rs_got(t, d, q).wait_send()
     rs_last(2, dxo)
     rs_last(3, dxo)
     for o, k in PEERS:
@@ -492,9 +511,9 @@
     for o, k in PEERS:
         dg_wait(o, k).wait_send()
     for t in range(2, 4):
-        for m in range(7):
-            for d in range(2):
-                rs_got(t, d, m).wait_send()
+        for q in range(NR):
+            for d in range(2):
+                rs_got(t, d, q).wait_send()
 
 
 def main(ridx, gates, x, dy, w1, w3, w2):
@@ -517,40 +536,26 @@
             pltpu.VMEM((NB, EL * RB, D), BF), pltpu.VMEM((NB, EL * RB, D), BF),
             pltpu.VMEM((EL, R, FF), BF), pltpu.VMEM((EL, R, FF), BF), pltpu.VMEM((EL, R, FF), BF),
             pltpu.VMEM((NB, EL * RB, 1), F32), pltpu.VMEM((NB, EL * RB, 1), F32),
-            pltpu.VMEM((4, ND, TOK, DH), F32), pltpu.VMEM((4, 8, TOK, DH), F32), pltpu.VMEM((4, 2, 7, HALF, DH), F32),
+            pltpu.VMEM((4, ND, TOK, DH), F32), pltpu.VMEM((4, 8, TOK, DH), F32), pltpu.VMEM((4, 2, NR, QR, DH), F32),
             pltpu.VMEM((ND, EL, 128), F32), pltpu.VMEM((ND, EL, 128), F32),
             dma(2, 2, LAST), dma(2, 2, LAST), dma(2, 2, LAST + 1), dma(2, 2, LAST + 1), dma(ND), dma(ND), dma(ND), dma(ND),
-            dma(4, 2, 7), dma(4, 2, 7), dma(4, 8), dma(4, 8),
+            dma(4, 2, NR), dma(4, 2, NR), dma(4, 8), dma(4, 8),
         ],
         compiler_params=pltpu.CompilerParams(vmem_limit_bytes=VMEM_LIMIT, collective_id=0, has_side_effects=True),
         name='moe',
     )(ridx, gates, x, dy, w1, w3, w2)
 
 
-def dw_kernel(y, dx, dg, x, do, a, du, dv, yo, dxo, dgo, g1, g3, g2, b1, b3, b2, sem):
-    e = pl.program_id(0)
-    slot = lax.rem(e, 2)
-    xb = x[...].reshape(NB * RB, D)
-    made = ((g1, b1, lambda: dot_tn(xb, du[0])), (g3, b3, lambda: dot_tn(xb, dv[0])),
-            (g2, b2, lambda: dot_tn(a[0], do[...].reshape(NB * RB, D))))
-    for i, (out, buf, make) in enumerate(made):
-        @pl.when(e >= 2)
-        def _():
-            pltpu.make_async_copy(buf.at[slot], out.at[e - 2], sem.at[i, slot]).wait()
-        buf[slot] = make()
-        pltpu.make_async_copy(buf.at[slot], out.at[e], sem.at[i, slot]).start()
-
-    @pl.when(e == 0)
+def dw_kernel(y, dx, dg, x, do, a, du, dv, yo, dxo, dgo, g1, g3, g2):
+    @pl.when(pl.program_id(0) == 0)
     def _():
         yo[...] = y[...]
         dxo[...] = dx[...]
         dgo[...] = dg[...]
-
-    @pl.when(e == EL - 1)
-    def _():
-        for i, (out, buf, make) in enumerate(made):
-            pltpu.make_async_copy(buf.at[1 - slot], out.at[e - 1], sem.at[i, 1 - slot]).wait()
-            pltpu.make_async_copy(buf.at[slot], out.at[e], sem.at[i, slot]).wait()
+    xb = x[...].reshape(NB * RB, D)
+    g1[0] = dot_tn(xb, du[0])
+    g3[0] = dot_tn(xb, dv[0])
+    g2[0] = dot_tn(a[0], do[...].reshape(NB * RB, D))
 
 
 def dw(y, dx, dg, xr, dor, ar, dur, dvr):
@@ -566,9 +571,8 @@
         out_shape=(sds((TOK, D), BF), sds((TOK, D), BF), sds((TOP, TOK), F32),
                    sds((EL, D, FF), F32), sds((EL, D, FF), F32), sds((EL, FF, D), F32)),
         in_specs=same + [br, br, act, act, act],
-        out_specs=same + [pl.BlockSpec(memory_space=pl.ANY)] * 3,
-        scratch_shapes=[pltpu.VMEM((2, D, FF), F32), pltpu.VMEM((2, D, FF), F32), pltpu.VMEM((2, FF, D), F32),
-                        pltpu.SemaphoreType.DMA((3, 2))],
+        out_specs=same + [pl.BlockSpec((1, D, FF), lambda e: (e, 0, 0)), pl.BlockSpec((1, D, FF), lambda e: (e, 0, 0)),
+                          pl.BlockSpec((1, FF, D), lambda e: (e, 0, 0))],
         name='dw',
     )(y, dx, dg, xr, dor, ar, dur, dvr)
 

time: 105 us -> 105 us (level)
  no operation moved by 1% of the time
where the time goes in v7:
time: 105 us; the launch traced here: 104 us
  Pallas kernels  103 us (98%)
    pallas_call x1, Pallas kernels, main(): pl.pallas_call(main_kernel, out_shape=(sds((TOK, D), BF), sds((TOK, D), B...  85.5 us
    pallas_call x1, Pallas kernels, dw(): pl.pallas_call(dw_kernel, grid=(EL,), out_shape=(sds((TOK, D), BF), sds((...  17.9 us

profile of v7, /device:TPU:0, one launch (start us, length us, event | category | flops | bytes accessed | tf_op | source)
XLA Modules:
  0.0 104.1 jit_solution(13756315588452657124)
XLA Ops:
  0.6 85.5 %moe.1 = (bf16[64,1024]{1,0:T(8,128)(2,1)}, bf16[64,1024]{1,0:T(8,128)(2,1)}, f32[8,64]{1,0:T(8,128)}, bf16[4,512,1024]{2,1,0:T(8,128)(2,1)}, bf16[4,512,1024]{2...) custom-call(s32[8,64]{1,0:T(8,128)} %bitcast.3, ...), custom_call_target="tpu_custom_call" | custom-call | tf_op jit(solution)/shard_map/moe/pallas_call | solution.py:525
  86.2 17.9 %dw.1 = (bf16[64,1024]{1,0:T(8,128)(2,1)}, bf16[64,1024]{1,0:T(8,128)(2,1)}, f32[8,64]{1,0:T(8,128)}, f32[8,1024,384]{2,1,0:T(8,128)}, f32[8,1024,384]{2,1,0:T(8,128)}, /*index=5*/f32[8,384,1024]{2,1,0:T(8,128)}) custom-call(bf16[64,1024]{1,0:T(8,128)(2,1)} %get-tuple-element.20.y, bf16[64,1024]{1,0:T(8,128)(2,1)} %get-tuple-element.21.dx, ...), custom_call_target="tpu_custom_call" | custom-call | tf_op jit(solution)/shard_map/dw/pallas_call | solution.py:568
